TPU v7x, 32 devices: a whole 2x2x4 slice. The times are simulated.
32 devices in a mesh: dp: 2 (over x), m: 4 (over z), bx: 4 (over y, core).
Axes of the slice: x: 2, y: 2, z: 4, core: 2. Of those that a mesh axis runs over, the one named last changes fastest.
Arguments:
- x_in: bfloat16 [8, 2048, 2048], P(('dp', 'bx'), None, 'm'), parts along dimension 0
- prompt_len: int32 [8], P(('dp', 'bx')), parts along dimension 0
- ln_scale: float32 [2, 2048], P(None, 'm')
- w_gate: bfloat16 [2, 2048, 16384], P(None, 'bx', 'm')
- w_up: bfloat16 [2, 2048, 16384], P(None, 'bx', 'm')
- w_q: bfloat16 [2, 2048, 8, 256], P(None, 'bx', 'm')
- w_k: bfloat16 [2, 2048, 256], P(None, 'bx')
- w_v: bfloat16 [2, 2048, 256], P(None, 'bx')
- w_down: bfloat16 [2, 16384, 2048], P(None, 'm', 'bx')
- w_o: bfloat16 [2, 8, 256, 2048], P(None, 'm', None, 'bx')
Outputs:
- output 1: bfloat16 [8, 2048, 2048], P(('dp', 'bx'), None, 'm'), parts along dimension 0
- output 2: bfloat16 [2, 8, 2048, 256], P(None, ('dp', 'bx')), parts along dimension 1
- output 3: bfloat16 [2, 8, 2048, 256], P(None, ('dp', 'bx')), parts along dimension 1
There are 2 independent parts. A program takes and returns all parts, laid end to end along the dimension named above; an argument that names none is the same for every part.
All inputs are finite; a program needn't handle non-finite values.
Results may differ from a plain program's by a relative error of at most 0.0138366.
Values are sent between devices in bfloat16 or wider.
A program may use at most 1 GiB of HBM per device.

v0:
```python
import jax
import jax.numpy as jnp
from jax import lax
from jax.sharding import PartitionSpec as P

NORM_EPS = 1e-6
ROPE_BASE = 10000.0


def rotary_tables(positions, head_dim):
    half_dim = head_dim // 2
    inv_freq = ROPE_BASE ** (-jnp.arange(half_dim, dtype=jnp.float32) * (2.0 / head_dim))
    angles = positions.astype(jnp.float32)[:, None] * inv_freq[None, :]
    return jnp.cos(angles), jnp.sin(angles)


def apply_rotary(values, cos_tab, sin_tab):
    half_dim = values.shape[-1] // 2
    first_half = values[..., :half_dim]
    second_half = values[..., half_dim:]
    return jnp.concatenate([first_half * cos_tab - second_half * sin_tab, second_half * cos_tab + first_half * sin_tab], axis=-1)


def masked_attention(queries, key_rows, val_rows, query_pos, key_pos, row_lens):
    score_scale = queries.shape[-1] ** -0.5
    scores = jnp.einsum('bthd,bsd->bhts', queries, key_rows, preferred_element_type=jnp.float32) * score_scale
    visible = (key_pos[None, None, None, :] <= query_pos[None, None, :, None]) & (key_pos[None, None, None, :] < row_lens[:, None, None, None])
    scores = jnp.where(visible, scores, -1e30)
    attn_probs = jax.nn.softmax(scores, axis=-1).astype(jnp.bfloat16)
    return jnp.einsum('bhts,bsd->bhtd', attn_probs, val_rows, preferred_element_type=jnp.float32).astype(jnp.bfloat16)


def solution(mesh):
    m_size = mesh.shape['m']
    batch_axes = ('dp', 'bx')
    row_spec = P(batch_axes, None, 'm')
    cache_spec = P(None, batch_axes, None, None)
    in_specs = (row_spec, P(batch_axes), P(None, 'm'), P(None, 'bx', 'm'), P(None, 'bx', 'm'), P(None, 'bx', 'm', None), P(None, 'bx', None), P(None, 'bx', None), P(None, 'm', 'bx'), P(None, 'm', None, 'bx'))

    def device_program(x_in, prompt_len, ln_scale, w_gate, w_up, w_q, w_k, w_v, w_down, w_o):
        embed_dim = x_in.shape[2] * m_size
        positions = jnp.arange(x_in.shape[1])
        cos_tab, sin_tab = rotary_tables(positions, w_k.shape[-1])
        hidden = x_in
        k_layers = []
        v_layers = []
        for layer_idx in range(w_gate.shape[0]):
            gate_full = lax.all_gather(w_gate[layer_idx], 'bx', axis=0, tiled=True)
            up_full = lax.all_gather(w_up[layer_idx], 'bx', axis=0, tiled=True)
            query_w = lax.all_gather(w_q[layer_idx], 'bx', axis=0, tiled=True)
            key_w = lax.all_gather(w_k[layer_idx], 'bx', axis=0, tiled=True)
            value_w = lax.all_gather(w_v[layer_idx], 'bx', axis=0, tiled=True)
            down_full = lax.all_gather(w_down[layer_idx], 'bx', axis=1, tiled=True)
            out_full = lax.all_gather(w_o[layer_idx], 'bx', axis=2, tiled=True)

            hidden_f32 = hidden.astype(jnp.float32)
            moments = jnp.stack([jnp.sum(hidden_f32, axis=-1), jnp.sum(hidden_f32 * hidden_f32, axis=-1)])
            moments = lax.psum(moments, 'm')
            row_mean = (moments[0] / embed_dim)[..., None]
            row_var = (moments[1] / embed_dim)[..., None] - row_mean * row_mean
            normed_part = ((hidden_f32 - row_mean) * lax.rsqrt(row_var + NORM_EPS) * ln_scale[layer_idx]).astype(jnp.bfloat16)
            normed = lax.all_gather(normed_part, 'm', axis=2, tiled=True)

            gate_proj = jnp.einsum('bte,ef->btf', normed, gate_full, preferred_element_type=jnp.float32)
            up_proj = jnp.einsum('bte,ef->btf', normed, up_full, preferred_element_type=jnp.float32)
            act_bf = (jax.nn.silu(gate_proj) * up_proj).astype(jnp.bfloat16)
            query_lin = jnp.einsum('bte,ehd->bthd', normed, query_w, preferred_element_type=jnp.float32)
            queries = apply_rotary(query_lin, cos_tab[:, None, :], sin_tab[:, None, :]).astype(jnp.bfloat16)
            key_lin = jnp.einsum('bte,ed->btd', normed, key_w, preferred_element_type=jnp.float32)
            key_rows = apply_rotary(key_lin, cos_tab, sin_tab).astype(jnp.bfloat16)
            val_rows = jnp.einsum('bte,ed->btd', normed, value_w, preferred_element_type=jnp.float32).astype(jnp.bfloat16)
            attn_out = masked_attention(queries, key_rows, val_rows, positions, positions, prompt_len)

            partial_sum = jnp.einsum('btf,fe->bte', act_bf, down_full, preferred_element_type=jnp.float32) + jnp.einsum('bhtd,hde->bte', attn_out, out_full, preferred_element_type=jnp.float32)
            reduced = lax.psum_scatter(partial_sum.astype(jnp.bfloat16), 'm', scatter_dimension=2, tiled=True)
            hidden = (hidden_f32 + reduced.astype(jnp.float32)).astype(jnp.bfloat16)
            k_layers.append(key_rows)
            v_layers.append(val_rows)
        return hidden, jnp.stack(k_layers), jnp.stack(v_layers)

    return jax.shard_map(device_program, mesh=mesh, in_specs=in_specs, out_specs=(row_spec, cache_spec, cache_spec), check_vma=False)
```

profile of v0, /device:TPU:0, one launch (start us, length us, event | category | flops | bytes accessed | tf_op | source)
XLA Modules:
  0.0 1511.6 jit_solution(9714732568762796243)
XLA Ops:
  11.6 20.5 %psum.14 = f32[2,1,2048]{2,1,0:T(1,128)S(1)} all-reduce(f32[2,1,2048]{2,1,0:T(1,128)S(1)} %pad_maximum_fusion.1), channel_id=1, replica_groups=mesh['dp'=2,'m'=4,'bx'=4] {'m'}, use_global_device_ids=true, to_apply=%region_2.0 | all-reduce | flops 4096 | bytes 32768 | tf_op jit(solution)/shard_map/psum | solution.py:58
  33.5 3.1 fusion.42
  40.5 6.1 fusion.124
  46.7 6.0 fusion.123
  52.8 6.0 fusion.122
  60.9 5.1 fusion.20
  65.9 3.7 multiply_cosine_fusion
  69.7 114.7 %all-gather.31.cloned.1.call-done = bf16[1,2048,2048]{2,1,0:T(8,128)(2,1)} async-done(((bf16[1,2048,512]{2,1,0:T(8,128)(2,1)}), bf16[1,2048,2048]{2,1,0:T(8,128)(2,1)}) %all-gather.31.cloned.1.call-update) | async-done | bytes 8388624 | tf_op jit(solution)/shard_map/all_gather | solution.py:62
  184.4 6.0 fusion.61
  190.4 4.2 fusion.94
  194.7 12.7 all-gather.43.cloned.1.call-done
  207.3 7.6 fusion.49
  217.1 16.8 %fusion.2 = (f32[2,2048]{1,0:T(2,128)S(1)}, f32[2048,2048,2]{1,0,2:T(8,128)}) fusion(pred[2048,2048]{0,1:T(8,128)(4,1)} %fusion.20, bf16[2048,2,128]{0,2,1:T(8,128)(2,1)} %get-tuple-element.20, bf16[2048,2,128]{0,2,1:T(8,128)(2,1)} %get-tuple-element.19, bf16[2048,128]{0,1:T(8,128)(2,1)S(1)} %bitcast.194, bf16[2048,128]{0,1:T(8,128)(2,1)S(1)} %bitcast.192), kind=kOutput, calls=%fused_computation.10 | convolution fusion | flops 4326420480 | bytes 40910848 | tf_op jit(solution)/shard_map/bthd,bsd->bhts/dot_general | solution.py:26
  234.0 15.0 fusion
  249.0 6.0 fusion.67
  255.0 18.3 %fusion.55 = bf16[2,2048,256]{2,1,0:T(8,128)(2,1)} fusion(f32[2,2048]{1,0:T(2,128)S(1)} %fusion, f32[2,2048]{1,0:T(2,128)S(1)} %get-tuple-element.41, f32[2048,2048,2]{1,0,2:T(8,128)} %get-tuple-element.42, pred[2048,2048]{0,1:T(8,128)(4,1)} %fusion.20, bf16[2048,256]{1,0:T(8,128)(2,1)S(1)} %fusion.67), kind=kOutput, calls=%fused_computation.70 | convolution fusion | flops 4337958912 | bytes 40927232 | tf_op jit(solution)/shard_map/bhts,bsd->bhtd/dot_general | solution.py:30
  273.3 60.4 %all-gather.35.cloned.1.call-done = bf16[1,2048,4096]{2,1,0:T(8,128)(2,1)} async-done(((bf16[1,512,4096]{2,1,0:T(8,128)(2,1)}), bf16[1,2048,4096]{2,1,0:T(8,128)(2,1)}) %all-gather.35.cloned.1.call-update) | async-done | bytes 16777232 | tf_op jit(solution)/shard_map/all_gather | solution.py:48
  333.7 43.9 %fusion.18 = f32[2048,4096]{1,0:T(8,128)} fusion(bf16[1,2048,4096]{2,1,0:T(8,128)(2,1)} %all-gather.35.cloned.1.call-done, bf16[1,2048,2048]{2,1,0:T(8,128)(2,1)} %all-gather.31.cloned.1.call-done), kind=kOutput, calls=%fused_computation.28 | convolution fusion | flops 34359738368 | bytes 58720256 | tf_op jit(solution)/shard_map/bte,ef->btf/dot_general | solution.py:64
  377.6 64.6 %all-gather.37.cloned.1.call-done = bf16[1,2048,4096]{2,1,0:T(8,128)(2,1)} async-done(((bf16[1,512,4096]{2,1,0:T(8,128)(2,1)}), bf16[1,2048,4096]{2,1,0:T(8,128)(2,1)}) %all-gather.37.cloned.1.call-update) | async-done | bytes 16777232 | tf_op jit(solution)/shard_map/all_gather | solution.py:49
  442.1 49.2 %multiply_convert_fusion.1 = bf16[2048,4096]{1,0:T(8,128)(2,1)} fusion(f32[2048,4096]{1,0:T(8,128)} %fusion.18, bf16[1,2048,4096]{2,1,0:T(8,128)(2,1)} %all-gather.37.cloned.1.call-done, bf16[1,2048,2048]{2,1,0:T(8,128)(2,1)} %all-gather.31.cloned.1.call-done), kind=kOutput, calls=%fused_computation.7 | convolution fusion | flops 34410070016 | bytes 75497472 | tf_op jit(solution)/shard_map/bte,ef->btf/dot_general | solution.py:65
  491.3 59.3 %all-gather.39.cloned.1.call-done = bf16[1,4096,2048]{2,1,0:T(8,128)(2,1)} async-done(((bf16[1,4096,512]{2,1,0:T(8,128)(2,1)}), bf16[1,4096,2048]{2,1,0:T(8,128)(2,1)}) %all-gather.39.cloned.1.call-update) | async-done | bytes 16777232 | tf_op jit(solution)/shard_map/all_gather | solution.py:53
  550.7 43.2 %fusion.15 = f32[2048,2048]{1,0:T(8,128)} fusion(bf16[2048,4096]{1,0:T(8,128)(2,1)} %multiply_convert_fusion.1, bf16[1,4096,2048]{2,1,0:T(8,128)(2,1)} %all-gather.39.cloned.1.call-done), kind=kOutput, calls=%fused_computation.25 | convolution fusion | flops 34359738368 | bytes 50331648 | tf_op jit(solution)/shard_map/btf,fe->bte/dot_general | solution.py:74
  593.9 10.7 fusion.37
  607.1 141.8 %reduce-scatter.3.cloned.1.call-done = bf16[1,2048,512]{2,1,0:T(8,128)(2,1)} async-done(((bf16[1,2048,2048]{2,1,0:T(8,128)(2,1)}), bf16[1,2048,512]{2,1,0:T(8,128)(2,1)}) %reduce-scatter.3.cloned.1.call-update) | async-done | bytes 2097168 | tf_op jit(solution)/shard_map/reduce_scatter | solution.py:75
  749.0 3.5 convert_reduce_fusion
  752.5 18.1 %psum.15 = f32[2,1,2048]{2,1,0:T(1,128)S(1)} all-reduce(f32[2,1,2048]{2,1,0:T(1,128)S(1)} %pad_maximum_fusion.2), channel_id=1, replica_groups=mesh['dp'=2,'m'=4,'bx'=4] {'m'}, use_global_device_ids=true, to_apply=%region_8.9 | all-reduce | flops 4096 | bytes 32768 | tf_op jit(solution)/shard_map/psum | solution.py:58
  770.7 3.1 fusion.47
  777.5 147.9 %all-gather.33.cloned.1.call-done = bf16[1,2048,2048]{2,1,0:T(8,128)(2,1)} async-done(((bf16[1,2048,512]{2,1,0:T(8,128)(2,1)}), bf16[1,2048,2048]{2,1,0:T(8,128)(2,1)}) %all-gather.33.cloned.1.call-update) | async-done | bytes 8388624 | tf_op jit(solution)/shard_map/all_gather | solution.py:62
  925.5 8.0 fusion.52
  935.3 6.5 all-gather.55.cloned.1.call-done
  941.8 6.0 fusion.64
  947.8 4.2 fusion.98
  952.1 16.3 %fusion.3 = (f32[2,2048]{1,0:T(2,128)S(1)}, f32[2048,2048,2]{1,0,2:T(8,128)}) fusion(pred[2048,2048]{0,1:T(8,128)(4,1)} %fusion.20, bf16[2048,2,128]{0,2,1:T(8,128)(2,1)S(1)} %copy-done.17, bf16[2048,2,128]{0,2,1:T(8,128)(2,1)S(1)} %get-tuple-element.17, bf16[2048,128]{0,1:T(8,128)(2,1)S(1)} %bitcast.198, bf16[2048,128]{0,1:T(8,128)(2,1)S(1)} %bitcast.196), kind=kOutput, calls=%fused_computation.11 | convolution fusion | flops 4326420480 | bytes 40910848 | tf_op jit(solution)/shard_map/bthd,bsd->bhts/dot_general | solution.py:26
  968.4 15.6 %fusion.1 = f32[2,2048]{1,0:T(2,128)} fusion(f32[2048,2048,2]{1,0,2:T(8,128)} %get-tuple-element.44, f32[2,2048]{1,0:T(2,128)S(1)} %get-tuple-element.43, pred[2048,2048]{0,1:T(8,128)(4,1)} %fusion.20), kind=kLoop, calls=%fused_computation.9 | loop fusion | flops 33550336 | bytes 37781504 | tf_op jit(solution)/shard_map/reduce_sum | solution.py:29
  984.0 66.3 %all-gather.49.cloned.1.call-done = bf16[1,2048,4096]{2,1,0:T(8,128)(2,1)} async-done(((bf16[1,512,4096]{2,1,0:T(8,128)(2,1)}), bf16[1,2048,4096]{2,1,0:T(8,128)(2,1)}) %all-gather.49.cloned.1.call-update) | async-done | bytes 16777232 | tf_op jit(solution)/shard_map/all_gather | solution.py:48
  1050.4 43.6 %fusion.10 = f32[2048,4096]{1,0:T(8,128)} fusion(bf16[1,2048,4096]{2,1,0:T(8,128)(2,1)} %all-gather.49.cloned.1.call-done, bf16[1,2048,2048]{2,1,0:T(8,128)(2,1)} %all-gather.33.cloned.1.call-done), kind=kOutput, calls=%fused_computation.19 | convolution fusion | flops 34359738368 | bytes 58720256 | tf_op jit(solution)/shard_map/bte,ef->btf/dot_general | solution.py:64
  1094.0 7.0 fusion.70
  1101.0 75.8 %all-gather.51.cloned.1.call-done = bf16[1,2048,4096]{2,1,0:T(8,128)(2,1)} async-done(((bf16[1,512,4096]{2,1,0:T(8,128)(2,1)}), bf16[1,2048,4096]{2,1,0:T(8,128)(2,1)}) %all-gather.51.cloned.1.call-update) | async-done | bytes 16777232 | tf_op jit(solution)/shard_map/all_gather | solution.py:49
  1176.8 49.2 %multiply_convert_fusion = bf16[2048,4096]{1,0:T(8,128)(2,1)} fusion(f32[2048,4096]{1,0:T(8,128)} %fusion.10, bf16[1,2048,4096]{2,1,0:T(8,128)(2,1)} %all-gather.51.cloned.1.call-done, bf16[1,2048,2048]{2,1,0:T(8,128)(2,1)} %all-gather.33.cloned.1.call-done), kind=kOutput, calls=%fused_computation.4 | convolution fusion | flops 34410070016 | bytes 75497472 | tf_op jit(solution)/shard_map/bte,ef->btf/dot_general | solution.py:65
  1226.0 59.2 %all-gather.53.cloned.1.call-done = bf16[1,4096,2048]{2,1,0:T(8,128)(2,1)} async-done(((bf16[1,4096,512]{2,1,0:T(8,128)(2,1)}), bf16[1,4096,2048]{2,1,0:T(8,128)(2,1)}) %all-gather.53.cloned.1.call-update) | async-done | bytes 16777232 | tf_op jit(solution)/shard_map/all_gather | solution.py:53
  1285.2 43.2 %fusion.7 = f32[2048,2048]{1,0:T(8,128)} fusion(bf16[2048,4096]{1,0:T(8,128)(2,1)} %multiply_convert_fusion, bf16[1,4096,2048]{2,1,0:T(8,128)(2,1)} %all-gather.53.cloned.1.call-done), kind=kOutput, calls=%fused_computation.16 | convolution fusion | flops 34359738368 | bytes 50331648 | tf_op jit(solution)/shard_map/btf,fe->bte/dot_general | solution.py:74
  1328.4 16.9 %fusion.58 = bf16[2,2048,256]{2,1,0:T(8,128)(2,1)S(1)} fusion(f32[2,2048]{1,0:T(2,128)S(1)} %copy-done.23, f32[2,2048]{1,0:T(2,128)S(1)} %copy-done.22, f32[2048,2048,2]{1,0,2:T(8,128)} %get-tuple-element.44, pred[2048,2048]{0,1:T(8,128)(4,1)} %fusion.20, bf16[2048,256]{1,0:T(8,128)(2,1)S(1)} %copy-done.16), kind=kOutput, calls=%fused_computation.71 | convolution fusion | flops 4337958912 | bytes 40927232 | tf_op jit(solution)/shard_map/bhts,bsd->bhtd/dot_general | solution.py:30
  1345.3 11.0 fusion.38
  1357.6 2.7 maximum_maximum_fusion
  1360.3 3.9 copy.19
  1364.2 3.1 pad_maximum_fusion
  1367.2 133.5 %reduce-scatter.5.cloned.1.call-done = bf16[1,2048,512]{2,1,0:T(8,128)(2,1)} async-done(((bf16[1,2048,2048]{2,1,0:T(8,128)(2,1)}), bf16[1,2048,512]{2,1,0:T(8,128)(2,1)}) %reduce-scatter.5.cloned.1.call-update) | async-done | bytes 2097168 | tf_op jit(solution)/shard_map/reduce_scatter | solution.py:75
  1500.7 3.5 fusion.48
  (117 shorter events, 22.6 us)
Async XLA Ops:
  7.2 29.5 %copy-start.13 = (bf16[2,512,2,256]{3,2,1,0:T(2,128)(2,1)S(1)}, bf16[2,512,2,256]{3,2,1,0:T(2,128)(2,1)}, u32[]{:S(2)}) copy-start(bf16[2,512,2,256]{3,2,1,0:T(2,128)(2,1)} %param.15) | copy-start | bytes 3145732
  7.2 32.5 %copy-start.18 = (bf16[2,512,256]{2,1,0:T(8,128)(2,1)S(1)}, bf16[2,512,256]{2,1,0:T(8,128)(2,1)}, u32[]{:S(2)}) copy-start(bf16[2,512,256]{2,1,0:T(8,128)(2,1)} %param.17) | copy-start | bytes 1572868
  7.2 62.5 %all-gather.41.cloned.1.call-start = ((), (), s32[]{:S(2)}) async-start(), calls=%async_computation.9 | async-start | bytes 1310720 | tf_op jit(solution)/shard_map/all_gather | solution.py:51
  9.2 175.2 %all-gather.31.cloned.1.call-start = ((), (), s32[]{:S(2)}) async-start(), calls=%async_computation.2 | async-start | bytes 10485760 | tf_op jit(solution)/shard_map/all_gather | solution.py:62
  36.6 170.8 %all-gather.43.cloned.1.call-start = ((), (), s32[]{:S(2)}) async-start(), calls=%async_computation.10 | async-start | bytes 2621440 | tf_op jit(solution)/shard_map/all_gather | solution.py:50
  39.6 209.4 %all-gather.45.cloned.1.call-start = ((), (), s32[]{:S(2)}) async-start(), calls=%async_computation.11 | async-start | bytes 1310720 | tf_op jit(solution)/shard_map/all_gather | solution.py:52
  40.5 293.2 %all-gather.35.cloned.1.call-start = ((), (), s32[]{:S(2)}) async-start(), calls=%async_computation.6 | async-start | bytes 20971520 | tf_op jit(solution)/shard_map/all_gather | solution.py:48
  46.6 395.5 %all-gather.37.cloned.1.call-start = ((), (), s32[]{:S(2)}) async-start(), calls=%async_computation.7 | async-start | bytes 20971520 | tf_op jit(solution)/shard_map/all_gather | solution.py:49
  52.7 6.1 copy-start.14
  52.7 497.9 %all-gather.39.cloned.1.call-start = ((), (), s32[]{:S(2)}) async-start(), calls=%async_computation.8 | async-start | bytes 20971520 | tf_op jit(solution)/shard_map/all_gather | solution.py:53
  58.8 535.1 %all-gather.47.cloned.1.call-start = ((), (), s32[]{:S(2)}) async-start(), calls=%async_computation.12 | async-start | bytes 2621440 | tf_op jit(solution)/shard_map/all_gather | solution.py:54
  59.9 689.0 %reduce-scatter.3.cloned.1.call-start = ((), (), s32[]{:S(2)}) async-start(), calls=%async_computation.3 | async-start | bytes 10485760 | tf_op jit(solution)/shard_map/reduce_scatter | solution.py:75
  60.2 130.2 %copy-start.25 = (f32[128]{0:T(128)}, f32[128]{0:T(128)S(1)}, u32[]{:S(2)}) copy-start(f32[128]{0:T(128)S(1)} %multiply_power_fusion) | copy-start | bytes 1540
  60.2 130.2 %copy-start.19 = (f32[2048]{0:T(1024)}, f32[2048]{0:T(1024)S(1)}, u32[]{:S(2)}) copy-start(f32[2048]{0:T(1024)S(1)} %iota_convert_fusion) | copy-start | bytes 24580
  69.6 145.3 %copy-start.2 = (f32[2048,128]{0,1:T(8,128)}, f32[2048,128]{0,1:T(8,128)S(1)}, u32[]{:S(2)}) copy-start(f32[2048,128]{0,1:T(8,128)S(1)} %get-tuple-element.37) | copy-start | bytes 3145732
  69.6 145.3 %copy-start.4 = (f32[2048,128]{0,1:T(8,128)}, f32[2048,128]{0,1:T(8,128)S(1)}, u32[]{:S(2)}) copy-start(f32[2048,128]{0,1:T(8,128)S(1)} %get-tuple-element.38) | copy-start | bytes 3145732
  194.7 22.5 %copy-start.7 = (bf16[1,2048,128]{1,2,0:T(8,128)(2,1)}, bf16[1,2048,128]{1,2,0:T(8,128)(2,1)S(1)}, u32[]{:S(2)}) copy-start(bf16[1,2048,128]{1,2,0:T(8,128)(2,1)S(1)} %get-tuple-element.23) | copy-start | bytes 1572868
  194.7 22.5 %copy-start.9 = (bf16[1,2048,128]{1,2,0:T(8,128)(2,1)}, bf16[1,2048,128]{1,2,0:T(8,128)(2,1)S(1)}, u32[]{:S(2)}) copy-start(bf16[1,2048,128]{1,2,0:T(8,128)(2,1)S(1)} %get-tuple-element.24) | copy-start | bytes 1572868
  255.0 18.3 %copy-start.15 = (bf16[2048,256]{1,0:T(8,128)(2,1)}, bf16[2048,256]{1,0:T(8,128)(2,1)S(1)}, u32[]{:S(2)}) copy-start(bf16[2048,256]{1,0:T(8,128)(2,1)S(1)} %fusion.67) | copy-start | bytes 3145732
  491.3 102.5 %copy-start.27 = (bf16[2,2048,256]{2,1,0:T(8,128)(2,1)S(1)}, bf16[2,2048,256]{2,1,0:T(8,128)(2,1)}, u32[]{:S(2)}) copy-start(bf16[2,2048,256]{2,1,0:T(8,128)(2,1)} %fusion.55) | copy-start | bytes 6291460
  604.6 1.0 copy-start.6
  604.6 144.4 %copy-start = (bf16[1,2048,512]{2,1,0:T(8,128)(2,1)S(1)}, bf16[1,2048,512]{2,1,0:T(8,128)(2,1)}, u32[]{:S(2)}) copy-start(bf16[1,2048,512]{2,1,0:T(8,128)(2,1)} %param.10) | copy-start | bytes 6291460
  604.6 166.1 %copy-start.24 = (f32[1,512]{1,0:T(1,128)S(1)}, f32[1,512]{1,0:T(1,128)}, u32[]{:S(2)}) copy-start(f32[1,512]{1,0:T(1,128)} %get-tuple-element.39) | copy-start | bytes 6148
  604.6 172.9 %all-gather.57.cloned.1.call-start = ((), (), s32[]{:S(2)}) async-start(), calls=%async_computation.17 | async-start | bytes 2621440 | tf_op jit(solution)/shard_map/all_gather | solution.py:50
  607.1 318.4 %all-gather.33.cloned.1.call-start = ((), (), s32[]{:S(2)}) async-start(), calls=%async_computation.4 | async-start | bytes 10485760 | tf_op jit(solution)/shard_map/all_gather | solution.py:62
  773.8 168.1 %all-gather.55.cloned.1.call-start = ((), (), s32[]{:S(2)}) async-start(), calls=%async_computation.16 | async-start | bytes 1310720 | tf_op jit(solution)/shard_map/all_gather | solution.py:51
  774.3 276.0 %all-gather.49.cloned.1.call-start = ((), (), s32[]{:S(2)}) async-start(), calls=%async_computation.13 | async-start | bytes 20971520 | tf_op jit(solution)/shard_map/all_gather | solution.py:48
  775.1 318.9 %all-gather.59.cloned.1.call-start = ((), (), s32[]{:S(2)}) async-start(), calls=%async_computation.18 | async-start | bytes 1310720 | tf_op jit(solution)/shard_map/all_gather | solution.py:52
  775.7 401.1 %all-gather.51.cloned.1.call-start = ((), (), s32[]{:S(2)}) async-start(), calls=%async_computation.14 | async-start | bytes 20971520 | tf_op jit(solution)/shard_map/all_gather | solution.py:49
  776.3 508.9 %all-gather.53.cloned.1.call-start = ((), (), s32[]{:S(2)}) async-start(), calls=%async_computation.15 | async-start | bytes 20971520 | tf_op jit(solution)/shard_map/all_gather | solution.py:53
  776.8 568.5 %all-gather.61.cloned.1.call-start = ((), (), s32[]{:S(2)}) async-start(), calls=%async_computation.19 | async-start | bytes 2621440 | tf_op jit(solution)/shard_map/all_gather | solution.py:54
  777.4 156.1 %copy-start.3 = (f32[2048,128]{0,1:T(8,128)S(1)}, f32[2048,128]{0,1:T(8,128)}, u32[]{:S(2)}) copy-start(f32[2048,128]{0,1:T(8,128)} %copy-done.2) | copy-start | bytes 3145732
  777.4 156.1 %copy-start.5 = (f32[2048,128]{0,1:T(8,128)S(1)}, f32[2048,128]{0,1:T(8,128)}, u32[]{:S(2)}) copy-start(f32[2048,128]{0,1:T(8,128)} %copy-done.4) | copy-start | bytes 3145732
  777.4 723.3 %reduce-scatter.5.cloned.1.call-start = ((), (), s32[]{:S(2)}) async-start(), calls=%async_computation.5 | async-start | bytes 10485760 | tf_op jit(solution)/shard_map/reduce_scatter | solution.py:75
  935.3 12.5 copy-start.20
  935.3 12.5 copy-start.26
  935.3 16.8 %copy-start.17 = (bf16[2048,2,128]{0,2,1:T(8,128)(2,1)S(1)}, bf16[2048,2,128]{0,2,1:T(8,128)(2,1)}, u32[]{:S(2)}) copy-start(bf16[2048,2,128]{0,2,1:T(8,128)(2,1)} %get-tuple-element.18) | copy-start | bytes 3145732
  952.1 16.3 %copy-start.11 = (bf16[1,2048,128]{1,2,0:T(8,128)(2,1)}, bf16[1,2048,128]{1,2,0:T(8,128)(2,1)S(1)}, u32[]{:S(2)}) copy-start(bf16[1,2048,128]{1,2,0:T(8,128)(2,1)S(1)} %get-tuple-element.21) | copy-start | bytes 1572868
  952.1 16.3 %copy-start.12 = (bf16[1,2048,128]{1,2,0:T(8,128)(2,1)}, bf16[1,2048,128]{1,2,0:T(8,128)(2,1)S(1)}, u32[]{:S(2)}) copy-start(bf16[1,2048,128]{1,2,0:T(8,128)(2,1)S(1)} %get-tuple-element.22) | copy-start | bytes 1572868
  968.4 15.7 %copy-start.21 = (f32[2,2048]{1,0:T(2,128)}, f32[2,2048]{1,0:T(2,128)S(1)}, u32[]{:S(2)}) copy-start(f32[2,2048]{1,0:T(2,128)S(1)} %get-tuple-element.43) | copy-start | bytes 49156
  1225.9 102.4 %copy-start.16 = (bf16[2048,256]{1,0:T(8,128)(2,1)S(1)}, bf16[2048,256]{1,0:T(8,128)(2,1)}, u32[]{:S(2)}) copy-start(bf16[2048,256]{1,0:T(8,128)(2,1)} %fusion.70) | copy-start | bytes 3145732
  1226.0 102.4 %copy-start.22 = (f32[2,2048]{1,0:T(2,128)S(1)}, f32[2,2048]{1,0:T(2,128)}, u32[]{:S(2)}) copy-start(f32[2,2048]{1,0:T(2,128)} %copy-done.21) | copy-start | bytes 49156
  1226.0 102.4 %copy-start.23 = (f32[2,2048]{1,0:T(2,128)S(1)}, f32[2,2048]{1,0:T(2,128)}, u32[]{:S(2)}) copy-start(f32[2,2048]{1,0:T(2,128)} %fusion.1) | copy-start | bytes 49156
  1356.4 1.0 copy-start.8
  1356.4 1.2 copy-start.10
  1356.4 144.3 %copy-start.1 = (bf16[1,2048,512]{2,1,0:T(8,128)(2,1)S(1)}, bf16[1,2048,512]{2,1,0:T(8,128)(2,1)}, u32[]{:S(2)}) copy-start(bf16[1,2048,512]{2,1,0:T(8,128)(2,1)} %get-tuple-element.10) | copy-start | bytes 6291460
Sparse Core Ops, SparseCore 0:
  9.6 19.2 all-gather.40
  36.7 147.6 all-gather.30
  186.6 20.7 all-gather.42
  208.8 16.4 all-gather.44
  226.7 106.9 all-gather.34
  335.1 106.9 all-gather.36
  443.7 106.9 all-gather.38
  552.2 22.3 all-gather.46
  604.7 144.1 reduce-scatter.2
  751.0 22.7 all-gather.56
  775.9 149.4 all-gather.32
  926.9 14.9 all-gather.54
  943.4 106.9 all-gather.48
  1051.8 16.4 all-gather.58
  1069.7 106.9 all-gather.50
  1178.2 106.9 all-gather.52
  1286.6 22.3 all-gather.60
  1356.5 144.1 reduce-scatter.4
where the time goes:
time: 1520 us; the launch traced here: 1510 us
  waiting for transfers between devices  946 us (62%)
  matrix products  403 us (27%)
  other arithmetic  73.1 us (5%)
  blocking collectives  38.7 us (3%)
  local copies, waits for them, and re-layouts  33.8 us (2%)
  between operations  15.9 us (1%)
    reduce_scatter x2, waiting for transfers between devices, device_program(): lax.psum_scatter(partial_sum.astype(jnp.bfloat16), 'm', scatter_dimension...  275 us
    all_gather x2, waiting for transfers between devices, device_program(): normed = lax.all_gather(normed_part, 'm', axis=2, tiled=True)  263 us
    all_gather x2, waiting for transfers between devices, device_program(): up_full = lax.all_gather(w_up[layer_idx], 'bx', axis=0, tiled=True)  140 us
    all_gather x2, waiting for transfers between devices, device_program(): gate_full = lax.all_gather(w_gate[layer_idx], 'bx', axis=0, tiled=True)  127 us
    all_gather x2, waiting for transfers between devices, device_program(): down_full = lax.all_gather(w_down[layer_idx], 'bx', axis=1, tiled=True)  119 us
    dot_general x2, matrix products, device_program(): jnp.einsum('bte,ef->btf', normed, up_full, preferred_element_type=jnp.flo...  98.4 us
    dot_general x2, matrix products, device_program(): jnp.einsum('bte,ef->btf', normed, gate_full, preferred_element_type=jnp.f...  87.5 us
    dot_general x2, matrix products, device_program(): jnp.einsum('btf,fe->bte', act_bf, down_full, preferred_element_type=jnp.f...  86.4 us
  transfers between devices with their start and end apart: 18, of which 12 were waited for; matrix products, arithmetic and copies ran while one was open for 32% of the time, Pallas kernels for 0%

commit v1 on v0

v1 whole, which is shorter than its diff:
```python
import functools

import jax
import jax.numpy as jnp
from jax import lax
from jax.experimental import pallas as pl
from jax.experimental.pallas import tpu as pltpu
from jax.sharding import PartitionSpec as P


NORM_EPS = 1e-6
ROPE_BASE = 10000.0
NUM_CHUNKS = 4
FFN_TILE = 512
VMEM_BYTES = 60 * 1024 * 1024


def rotary_tables(positions, head_dim):
    half_dim = head_dim // 2
    inv_freq = ROPE_BASE ** (-jnp.arange(half_dim, dtype=jnp.float32) * (2.0 / head_dim))
    angles = positions.astype(jnp.float32)[:, None] * inv_freq[None, :]
    return jnp.cos(angles), jnp.sin(angles)


def row_offsets(me, group, rows):
    half = rows // 2
    other = me ^ 1
    far = me ^ 2
    far_other = me ^ 3
    return (
        me * rows,
        other * rows,
        far * rows + group * half,
        far * rows + (1 - group) * half,
        far_other * rows + group * half,
        far_other * rows + (1 - group) * half,
    )


def piece_copies(pieces, dst, offsets, cols, sem):
    copies = []
    for piece, offset in zip(pieces, offsets):
        rows = piece.shape[0]
        copies.append(pltpu.make_async_copy(piece.at[:, cols], dst.at[pl.ds(pl.multiple_of(offset, rows), rows)], sem))
    return copies


def qkv_body(place, x_ref, ln_ref, cos_ref, sin_ref, *refs, head_dim, num_q, split):
    pieces = refs[:6]
    h_ref, q_ref, k_ref, v_ref, w_full, sem = refs[6:]
    offsets = row_offsets(place[0], place[1], pieces[0].shape[0])
    out_dim = w_full.shape[1]
    copies = piece_copies(pieces, w_full, offsets, slice(0, out_dim), sem)
    for copy in copies:
        copy.start()
    tokens, _ = h_ref.shape
    step = min(128, tokens)

    def norm_step(i, carry):
        rows = pl.ds(pl.multiple_of(i * step, step), step)
        if split:
            x = jnp.concatenate([x_ref[j, rows, :] for j in range(x_ref.shape[0])], axis=-1).astype(jnp.float32)
        else:
            x = x_ref[rows, :].astype(jnp.float32)
        mean = jnp.mean(x, axis=-1, keepdims=True)
        centered = x - mean
        var = jnp.mean(centered * centered, axis=-1, keepdims=True)
        h_ref[rows, :] = (centered * lax.rsqrt(var + NORM_EPS) * ln_ref[...]).astype(jnp.bfloat16)
        return carry

    lax.fori_loop(0, tokens // step, norm_step, 0)
    for copy in copies:
        copy.wait()
    half = head_dim // 2
    cos = cos_ref[...]
    sin = sin_ref[...]
    h = h_ref[...]
    for i in range(num_q + 2):
        lin = jnp.dot(h, w_full[:, i * head_dim:(i + 1) * head_dim], preferred_element_type=jnp.float32)
        if i == num_q + 1:
            v_ref[...] = lin.astype(jnp.bfloat16)
            continue
        u1 = lin[:, :half]
        u2 = lin[:, half:]
        lo = (u1 * cos - u2 * sin).astype(jnp.bfloat16)
        hi = (u2 * cos + u1 * sin).astype(jnp.bfloat16)
        if i < num_q:
            q_ref[:, i * head_dim:i * head_dim + half] = lo
            q_ref[:, i * head_dim + half:(i + 1) * head_dim] = hi
        else:
            k_ref[:, :half] = lo
            k_ref[:, half:] = hi


def qkv_call(place, x_chunk, ln_row, cos, sin, pieces, head_dim, num_q):
    split = x_chunk.ndim == 3
    tokens = x_chunk.shape[-2]
    embed = ln_row.shape[1]
    out_dim = (num_q + 2) * head_dim
    full = lambda shape: pl.BlockSpec(shape, lambda i, s: (0,) * len(shape))
    anyspec = pl.BlockSpec(memory_space=pl.ANY)
    bf16 = jnp.bfloat16
    return pl.pallas_call(
        functools.partial(qkv_body, head_dim=head_dim, num_q=num_q, split=split),
        grid_spec=pltpu.PrefetchScalarGridSpec(
            num_scalar_prefetch=1,
            grid=(1,),
            in_specs=[full(x_chunk.shape), full(ln_row.shape), full(cos.shape), full(sin.shape)] + [anyspec] * 6,
            out_specs=[full((tokens, embed)), full((tokens, num_q * head_dim)), full((tokens, head_dim)), full((tokens, head_dim))],
            scratch_shapes=[pltpu.VMEM((embed, out_dim), bf16), pltpu.SemaphoreType.DMA],
        ),
        out_shape=[
            jax.ShapeDtypeStruct((tokens, embed), bf16),
            jax.ShapeDtypeStruct((tokens, num_q * head_dim), bf16),
            jax.ShapeDtypeStruct((tokens, head_dim), bf16),
            jax.ShapeDtypeStruct((tokens, head_dim), bf16),
        ],
        compiler_params=pltpu.CompilerParams(vmem_limit_bytes=VMEM_BYTES),
        cost_estimate=pl.CostEstimate(flops=2 * tokens * embed * out_dim * 2, bytes_accessed=2 * (2 * tokens * embed + embed * out_dim), transcendentals=0),
        name="qkv",
    )(place, x_chunk, ln_row, cos, sin, *pieces)


def attn_body(lens, q_ref, *refs, head_dim, num_q, block):
    num_kv = (len(refs) - 1) // 2
    k_refs = refs[:num_kv]
    v_refs = refs[num_kv:2 * num_kv]
    o_ref = refs[2 * num_kv]
    tokens = q_ref.shape[0]
    scale = head_dim ** -0.5
    row_len = lens[0]
    last = num_kv - 1

    for head in range(num_q):
        cols = slice(head * head_dim, (head + 1) * head_dim)
        for qi in range(tokens // block):
            q = q_ref[qi * block:(qi + 1) * block, cols]
            scores = []
            for j in range(num_kv):
                width = tokens if j < last else (qi + 1) * block
                s = lax.dot_general(q, k_refs[j][:width, :], (((1,), (1,)), ((), ())), preferred_element_type=jnp.float32) * scale
                key_row = j * tokens + lax.broadcasted_iota(jnp.int32, (1, width), 1)
                if j < last:
                    visible = jnp.broadcast_to(key_row < row_len, s.shape)
                else:
                    key_pos = lax.broadcasted_iota(jnp.int32, s.shape, 1)
                    query_pos = qi * block + lax.broadcasted_iota(jnp.int32, s.shape, 0)
                    visible = (key_pos <= query_pos) & (key_row < row_len)
                scores.append(jnp.where(visible, s, -1e30))
            top = functools.reduce(jnp.maximum, [jnp.max(s, axis=-1, keepdims=True) for s in scores])
            weights = [jnp.exp(s - top) for s in scores]
            total = functools.reduce(jnp.add, [jnp.sum(w, axis=-1, keepdims=True) for w in weights])
            inverse = 1.0 / total
            out = None
            for j, w in enumerate(weights):
                part = jnp.dot((w * inverse).astype(jnp.bfloat16), v_refs[j][:w.shape[1], :], preferred_element_type=jnp.float32)
                out = part if out is None else out + part
            o_ref[qi * block:(qi + 1) * block, cols] = out.astype(jnp.bfloat16)


def attn_call(row_len, queries, keys, values, head_dim, num_q):
    tokens = queries.shape[0]
    num_kv = len(keys)
    full = lambda shape: pl.BlockSpec(shape, lambda i, s: (0,) * len(shape))
    return pl.pallas_call(
        functools.partial(attn_body, head_dim=head_dim, num_q=num_q, block=min(256, tokens)),
        grid_spec=pltpu.PrefetchScalarGridSpec(
            num_scalar_prefetch=1,
            grid=(1,),
            in_specs=[full(queries.shape)] + [full(keys[0].shape)] * (2 * num_kv),
            out_specs=full(queries.shape),
        ),
        out_shape=jax.ShapeDtypeStruct(queries.shape, jnp.bfloat16),
        compiler_params=pltpu.CompilerParams(vmem_limit_bytes=VMEM_BYTES),
        cost_estimate=pl.CostEstimate(flops=8 * num_q * tokens * tokens * num_kv * head_dim, bytes_accessed=4 * tokens * num_q * head_dim, transcendentals=num_q * tokens * tokens * num_kv),
        name="attn",
    )(row_len, queries, *keys, *values)


def ffn_body(place, h_ref, base_ref, *refs, tile, first, split_out):
    gate_p, up_p, down_p = refs[:6], refs[6:12], refs[12:18]
    refs = refs[18:]
    out_p = ()
    if first:
        out_p, refs = refs[:6], refs[6:]
    y_ref, gate_w, up_w, down_w, acc, sems = refs[:6]
    me = place[0]
    group = place[1]
    block = down_p[0].shape[1]
    ffn = down_p[0].shape[0]
    steps = ffn // tile
    half_steps = steps // 2
    offsets = row_offsets(me, group, gate_p[0].shape[0])
    blocks = [pl.ds(pl.multiple_of((me ^ i) * block, block), block) for i in range(4)]
    start = lambda copy: copy.start()
    wait = lambda copy: copy.wait()

    def fetch(f, slot, go):
        sem = sems.at[slot]
        cols = pl.ds(pl.multiple_of(f * tile, tile), tile)
        copies = piece_copies(gate_p, gate_w.at[slot], offsets, cols, sem)
        copies += piece_copies(up_p, up_w.at[slot], offsets, cols, sem)
        copies.append(pltpu.make_async_copy(down_p[0].at[cols], down_w.at[slot, :, blocks[0]], sem))
        copies.append(pltpu.make_async_copy(down_p[1].at[cols], down_w.at[slot, :, blocks[1]], sem))
        for copy in copies:
            go(copy)
        part = f // half_steps
        rows = pl.ds(pl.multiple_of((f - part * half_steps) * tile, tile), tile)
        for which in range(2):
            want = group if which == 0 else 1 - group

            @pl.when(part == want)
            def _():
                go(pltpu.make_async_copy(down_p[2 + which].at[rows], down_w.at[slot, :, blocks[2]], sem))
                go(pltpu.make_async_copy(down_p[4 + which].at[rows], down_w.at[slot, :, blocks[3]], sem))

    if first:
        out_w, out_sem = refs[6:]
        half = out_p[2].shape[0]
        near = pl.ds(pl.multiple_of(group * half, half), half)
        away = pl.ds(pl.multiple_of((1 - group) * half, half), half)
        out_copies = [
            pltpu.make_async_copy(out_p[0], out_w.at[:, blocks[0]], out_sem),
            pltpu.make_async_copy(out_p[1], out_w.at[:, blocks[1]], out_sem),
            pltpu.make_async_copy(out_p[2], out_w.at[near, blocks[2]], out_sem),
            pltpu.make_async_copy(out_p[3], out_w.at[away, blocks[2]], out_sem),
            pltpu.make_async_copy(out_p[4], out_w.at[near, blocks[3]], out_sem),
            pltpu.make_async_copy(out_p[5], out_w.at[away, blocks[3]], out_sem),
        ]
        for copy in out_copies:
            copy.start()
        fetch(0, 0, start)
        for copy in out_copies:
            copy.wait()
        acc[...] = jnp.dot(base_ref[...], out_w[...], preferred_element_type=jnp.float32)
    else:
        fetch(0, 0, start)
        acc[...] = base_ref[...]

    def step(f, carry):
        slot = lax.rem(f, 2)
        fetch(f, slot, wait)

        @pl.when(f + 1 < steps)
        def _():
            fetch(f + 1, 1 - slot, start)

        h = h_ref[...]
        gate = jnp.dot(h, gate_w[slot], preferred_element_type=jnp.float32)
        up = jnp.dot(h, up_w[slot], preferred_element_type=jnp.float32)
        act = (gate * jax.nn.sigmoid(gate) * up).astype(jnp.bfloat16)
        acc[...] += jnp.dot(act, down_w[slot], preferred_element_type=jnp.float32)
        return carry

    lax.fori_loop(0, steps, step, 0)
    if split_out:
        part = y_ref.shape[2]
        for j in range(y_ref.shape[0]):
            y_ref[j] = acc[:, j * part:(j + 1) * part].astype(y_ref.dtype)
    else:
        y_ref[...] = acc[...].astype(y_ref.dtype)


def ffn_call(place, normed, base, gate_p, up_p, down_p, out_p, split):
    first = out_p is not None
    tokens, embed = normed.shape
    ffn = down_p[0].shape[0]
    tile = min(FFN_TILE, ffn // 2)
    full = lambda shape: pl.BlockSpec(shape, lambda i, s: (0,) * len(shape))
    anyspec = pl.BlockSpec(memory_space=pl.ANY)
    bf16 = jnp.bfloat16
    out_dims = (split, tokens, embed // split) if split else (tokens, embed)
    scratch = [
        pltpu.VMEM((2, embed, tile), bf16),
        pltpu.VMEM((2, embed, tile), bf16),
        pltpu.VMEM((2, tile, embed), bf16),
        pltpu.VMEM((tokens, embed), jnp.float32),
        pltpu.SemaphoreType.DMA((2,)),
    ]
    if first:
        scratch += [pltpu.VMEM((base.shape[1], embed), bf16), pltpu.SemaphoreType.DMA]
    pieces = [*gate_p, *up_p, *down_p] + (list(out_p) if first else [])
    return pl.pallas_call(
        functools.partial(ffn_body, tile=tile, first=first, split_out=bool(split)),
        grid_spec=pltpu.PrefetchScalarGridSpec(
            num_scalar_prefetch=1,
            grid=(1,),
            in_specs=[full(normed.shape), full(base.shape)] + [anyspec] * len(pieces),
            out_specs=full(out_dims),
            scratch_shapes=scratch,
        ),
        out_shape=jax.ShapeDtypeStruct(out_dims, jnp.float32 if first else bf16),
        compiler_params=pltpu.CompilerParams(vmem_limit_bytes=VMEM_BYTES),
        cost_estimate=pl.CostEstimate(flops=2 * tokens * embed * 3 * ffn, bytes_accessed=2 * (2 * tokens * embed + 3 * ffn * embed), transcendentals=tokens * ffn),
    )(place, normed, base, *pieces)


def solution(mesh):
    m_size = mesh.shape['m']
    batch_axes = ('dp', 'bx')
    row_spec = P(batch_axes, None, 'm')
    cache_spec = P(None, batch_axes, None, None)
    in_specs = (row_spec, P(batch_axes), P(None, 'm'), P(None, 'bx', 'm'), P(None, 'bx', 'm'), P(None, 'bx', 'm', None), P(None, 'bx', None), P(None, 'bx', None), P(None, 'm', 'bx'), P(None, 'm', None, 'bx'))
    far_perm = [(b, b ^ 2) for b in range(4)]
    near_perm = [(b, b ^ 1) for b in range(4)]
    swap_perm = [(0, 1), (1, 0)]

    def spread(own, group):
        half = own.shape[0] // 2
        part = lax.dynamic_slice_in_dim(own, group * half, half, axis=0)
        far_a = lax.ppermute(part, 'bx', far_perm)
        far_b = lax.ppermute(far_a, 'dp', swap_perm)
        near = lax.ppermute(own, 'bx', near_perm)
        far_near_a = lax.ppermute(far_a, 'bx', near_perm)
        far_near_b = lax.ppermute(far_b, 'bx', near_perm)
        return own, near, far_a, far_b, far_near_a, far_near_b

    def gather_rows(own, col):
        pair = [(0, 1), (1, 0), (2, 3), (3, 2)]
        middle = [(1, 2), (2, 1)]
        outward = [(1, 0), (2, 3)]
        mate = lax.ppermute(own, 'm', pair)
        mid_own = lax.ppermute(own, 'm', middle)
        mid_mate = lax.ppermute(mate, 'm', middle)
        end_own = lax.ppermute(mid_own, 'm', outward)
        end_mate = lax.ppermute(mid_mate, 'm', outward)
        inner = (col == 1) | (col == 2)
        far_own = jnp.where(inner, mid_own, end_own)
        far_mate = jnp.where(inner, mid_mate, end_mate)
        pick = lambda a, b, c, d: jnp.where(col == 0, a, jnp.where(col == 1, b, jnp.where(col == 2, c, d)))
        return jnp.concatenate([
            pick(own, mate, far_mate, far_mate),
            pick(mate, own, far_own, far_own),
            pick(far_own, far_own, own, mate),
            pick(far_mate, far_mate, mate, own),
        ], axis=0)

    def layers(x_in, prompt_len, ln_scale, w_gate, w_up, w_q, w_k, w_v, w_down, w_o):
        x_own = x_in[0]
        seq, part_dim = x_own.shape
        embed = part_dim * m_size
        head_dim = w_k.shape[-1]
        num_q = w_q.shape[2]
        num_layers = w_gate.shape[0]
        tokens = seq // NUM_CHUNKS
        share = tokens // m_size
        half_ffn = w_gate.shape[2] // 2
        me = lax.axis_index('bx')
        group = lax.axis_index('dp')
        col = lax.axis_index('m')
        place = jnp.stack([me, group]).astype(jnp.int32)

        cos_tab, sin_tab = rotary_tables(jnp.arange(seq), head_dim)
        ln_full = lax.all_gather(ln_scale, 'm', axis=1, tiled=True)
        chunks = [lax.all_gather(x_own[c * tokens:(c + 1) * tokens], 'm', axis=0) for c in range(NUM_CHUNKS)]

        pieces = []
        for l in range(num_layers):
            own = {
                'qkv': jnp.concatenate([w_q[l].reshape(w_q.shape[1], -1), w_k[l], w_v[l]], axis=1),
                'out': w_o[l].reshape(-1, w_o.shape[-1]),
                'ga': w_gate[l, :, :half_ffn],
                'ua': w_up[l, :, :half_ffn],
                'da': w_down[l, :half_ffn],
                'gb': w_gate[l, :, half_ffn:],
                'ub': w_up[l, :, half_ffn:],
                'db': w_down[l, half_ffn:],
            }
            pieces.append({k: spread(v, group) for k, v in own.items()})

        def head(l, c, keys, values):
            rows = slice(c * tokens, (c + 1) * tokens)
            normed, q, k, v = qkv_call(place, chunks[c], ln_full[l:l + 1], cos_tab[rows], sin_tab[rows], pieces[l]['qkv'], head_dim, num_q)
            keys.append(k)
            values.append(v)
            return normed, attn_call(prompt_len, q, keys, values, head_dim, num_q)

        def ffn(l, normed, attn_out):
            w = pieces[l]
            half_sum = ffn_call(place, normed, attn_out, w['ga'], w['ua'], w['da'], w['out'], 0)
            return ffn_call(place, normed, half_sum, w['gb'], w['ub'], w['db'], None, m_size if l == 1 else 0)

        keys0, values0, keys1, values1 = [], [], [], []
        rows1 = []
        for c in range(NUM_CHUNKS):
            normed, attn_out = head(0, c, keys0, values0)
            partial = ffn(0, normed, attn_out)
            reduced = lax.psum_scatter(partial, 'm', scatter_dimension=0, tiled=True)
            before = lax.dynamic_slice_in_dim(chunks[c], col * share, share, axis=1)
            before = before.transpose(1, 0, 2).reshape(share, embed)
            y_rows = (before.astype(jnp.float32) + reduced.astype(jnp.float32)).astype(jnp.bfloat16)
            rows1.append(gather_rows(y_rows, col))
        chunks = rows1
        outs = []
        for c in range(NUM_CHUNKS):
            normed, attn_out = head(1, c, keys1, values1)
            partial = ffn(1, normed, attn_out)
            reduced = lax.psum_scatter(partial, 'm', scatter_dimension=0, tiled=True)
            before = lax.dynamic_slice_in_dim(chunks[c], col * part_dim, part_dim, axis=1)
            outs.append((before.astype(jnp.float32) + reduced[0].astype(jnp.float32)).astype(jnp.bfloat16))
        hidden = jnp.concatenate(outs, axis=0)[None]
        k_cache = jnp.stack([jnp.concatenate(keys0, axis=0), jnp.concatenate(keys1, axis=0)])[:, None]
        v_cache = jnp.stack([jnp.concatenate(values0, axis=0), jnp.concatenate(values1, axis=0)])[:, None]
        return hidden, k_cache, v_cache

    return jax.shard_map(layers, mesh=mesh, in_specs=in_specs, out_specs=(row_spec, cache_spec, cache_spec), check_vma=False)
```

time: 1520 us -> 1100 us (0.72)
  waiting for transfers between devices: 946 us -> 426 us
  Pallas kernels: 0 us -> 464 us
  matrix products: 403 us -> 0 us
  starting transfers between devices: 0.9 us -> 78.6 us
  other arithmetic: 73.1 us -> 40.8 us
  blocking collectives: 38.7 us -> 14.6 us
  local copies, waits for them, and re-layouts: 33.8 us -> 51.3 us
    all_gather x16 -> x4, waiting for transfers between devices: 668 us -> 0.05 us  [layers(): lax.all_gather(x_own[c * tokens:(c + 1) * tokens], 'm', axis=0)]
    pallas_call x0 -> x32, Pallas kernels: none -> 464 us  [the longest x16 362 us: ffn_call(): pl.pallas_call(functools.partial(ffn_body, tile=tile, first=first, split_...]
    dot_general x18 -> x0, matrix products: 403 us -> none  [the longest x2 98.4 us: device_program(): jnp.einsum('bte,ef->btf', normed, up_full, preferred_element_type=jnp.flo...]
    ppermute x0 -> x100, waiting for transfers between devices: none -> 381 us  [the longest x16 217 us: spread(): far_a = lax.ppermute(part, 'bx', far_perm)]
    reduce_scatter x2 -> x8, waiting for transfers between devices: 275 us -> 43.7 us  [layers(): reduced = lax.psum_scatter(partial, 'm', scatter_dimension=0, tiled=True)]
    ppermute x0 -> x100, starting transfers between devices: none -> 78.1 us  [the longest x16 21.6 us: spread(): far_a = lax.ppermute(part, 'bx', far_perm)]
    psum x2 -> x0, blocking collectives: 38.7 us -> none  [device_program(): moments = lax.psum(moments, 'm')]
    reduce_sum x4 -> x0, other arithmetic: 36.5 us -> none  [the longest x2 30.7 us: masked_attention(): attn_probs = jax.nn.softmax(scores, axis=-1).astype(jnp.bfloat16)]
  transfers between devices with their start and end apart: 18 -> 112, of which waited for: 12 -> 32; matrix products, arithmetic and copies ran while one was open for 32% -> 7% of each run, Pallas kernels for 0% -> 39%
where the time goes in v1:
time: 1100 us; the launch traced here: 1090 us
  Pallas kernels  464 us (42%)
  waiting for transfers between devices  426 us (39%)
  starting transfers between devices  78.6 us (7%)
  local copies, waits for them, and re-layouts  51.3 us (5%)
  other arithmetic  40.8 us (4%)
  between operations  16.3 us (1%)
  blocking collectives  14.6 us (1%)
    pallas_call x16, Pallas kernels, ffn_call(): pl.pallas_call(functools.partial(ffn_body, tile=tile, first=first, split_...  362 us
    ppermute x16, waiting for transfers between devices, spread(): far_a = lax.ppermute(part, 'bx', far_perm)  217 us
    ppermute x16, waiting for transfers between devices, spread(): far_b = lax.ppermute(far_a, 'dp', swap_perm)  76.9 us
    pallas_call x8, Pallas kernels, qkv_call(): pl.pallas_call(functools.partial(qkv_body, head_dim=head_dim, num_q=num_q...  61.3 us
    reduce_scatter x8, waiting for transfers between devices, layers(): reduced = lax.psum_scatter(partial, 'm', scatter_dimension=0, tiled=True)  43.7 us
    pallas_call x8, Pallas kernels, attn_call(): pl.pallas_call(functools.partial(attn_body, head_dim=head_dim, num_q=num_...  40.9 us
    ppermute x4, waiting for transfers between devices, gather_rows(): end_own = lax.ppermute(mid_own, 'm', outward)  40.9 us
    ppermute x4, waiting for transfers between devices, gather_rows(): end_mate = lax.ppermute(mid_mate, 'm', outward)  36.1 us
  transfers between devices with their start and end apart: 112, of which 32 were waited for; matrix products, arithmetic and copies ran while one was open for 7% of the time, Pallas kernels for 39%

profile of v1, /device:TPU:0, one launch (start us, length us, event | category | flops | bytes accessed | tf_op | source)
XLA Modules:
  0.0 1091.3 jit_solution(16155632226840318127)
XLA Ops:
  38.2 8.3 fusion.5
  47.1 8.2 fusion.4
  59.5 10.0 collective-permute-done.2.refs_3_
  73.3 9.9 collective-permute-done.11.refs_8_
  85.1 20.5 %collective-permute-done.16.refs_14_ = bf16[1024,512]{1,0:T(8,128)(2,1)S(1)} collective-permute-done((bf16[1024,512]{1,0:T(8,128)(2,1)S(1)}, bf16[1024,512]{1,0:T(8,128)(2,1)S(1)}, u32[]{:S(2)}, u32[]{:S(2)}) %collective-permute-start.16) | collective-permute-done | bytes 1048608 | tf_op jit(solution)/shard_map/ppermute | solution.py:311
  105.6 22.6 %collective-permute-done.26.refs_2_ = bf16[256,2048]{1,0:T(8,128)(2,1)} collective-permute-done((bf16[256,2048]{1,0:T(8,128)(2,1)S(1)}, bf16[256,2048]{1,0:T(8,128)(2,1)}, u32[]{:S(2)}, u32[]{:S(2)}) %collective-permute-start.26) | collective-permute-done | bytes 1048608 | tf_op jit(solution)/shard_map/ppermute | solution.py:311
  130.0 20.6 %collective-permute-done.31.refs_8_ = bf16[256,2048]{1,0:T(8,128)(2,1)} collective-permute-done((bf16[256,2048]{1,0:T(8,128)(2,1)S(1)}, bf16[256,2048]{1,0:T(8,128)(2,1)}, u32[]{:S(2)}, u32[]{:S(2)}) %collective-permute-start.31) | collective-permute-done | bytes 1048608 | tf_op jit(solution)/shard_map/ppermute | solution.py:311
  150.6 22.1 %collective-permute-done.36.refs_14_ = bf16[1024,512]{1,0:T(8,128)(2,1)S(1)} collective-permute-done((bf16[1024,512]{1,0:T(8,128)(2,1)S(1)}, bf16[1024,512]{1,0:T(8,128)(2,1)S(1)}, u32[]{:S(2)}, u32[]{:S(2)}) %collective-permute-start.36) | collective-permute-done | bytes 1048608 | tf_op jit(solution)/shard_map/ppermute | solution.py:311
  178.5 22.6 %collective-permute-done.12.refs_9_ = bf16[256,2048]{1,0:T(8,128)(2,1)} collective-permute-done((bf16[256,2048]{1,0:T(8,128)(2,1)}, bf16[256,2048]{1,0:T(8,128)(2,1)}, u32[]{:S(2)}, u32[]{:S(2)}) %collective-permute-start.12) | collective-permute-done | bytes 1048608 | tf_op jit(solution)/shard_map/ppermute | solution.py:312
  204.1 14.6 %all_gather.20 = f32[2,2048]{1,0:T(2,128)S(1)} all-gather(f32[2,512]{1,0:T(2,128)S(1)} %copy-done.35), channel_id=1, replica_groups=mesh['dp'=2,'m'=4,'bx'=4] {'m'}, dimensions={1}, use_global_device_ids=true | all-gather | bytes 20480 | tf_op jit(solution)/shard_map/all_gather | solution.py:354
  230.8 7.6 qkv.14
  238.4 7.8 qkv.8
  251.9 20.5 %collective-permute-done.32.refs_9_ = bf16[256,2048]{1,0:T(8,128)(2,1)} collective-permute-done((bf16[256,2048]{1,0:T(8,128)(2,1)}, bf16[256,2048]{1,0:T(8,128)(2,1)}, u32[]{:S(2)}, u32[]{:S(2)}) %collective-permute-start.32) | collective-permute-done | bytes 1048608 | tf_op jit(solution)/shard_map/ppermute | solution.py:312
  272.9 7.6 qkv.10
  280.6 7.6 qkv.12
  296.1 23.2 %shard_map.133.base_ref = f32[512,2048]{1,0:T(8,128)} custom-call(s32[2]{0:T(128)} %pad_add_fusion.place, bf16[512,2048]{1,0:T(8,128)(2,1)} %get-tuple-element.59.h_ref, bf16[512,512]{1,0:T(8,128)(2,1)} %attn.14.base_ref, bf16[512,2048]{1,0:T(8,128)(2,1)} %get-tuple-element.90.refs_0_, bf16[512,2048]{1,0:T(8,128)(2,1)} %collective-permute-done.5.refs_1_, ...), custom_call_target="tpu_custom_call" | custom-call | flops 12884901888 | bytes 29360128 | tf_op jit(solution)/shard_map/pallas_call | solution.py:283
  319.3 21.9 %shard_map.134 = bf16[512,2048]{1,0:T(8,128)(2,1)} custom-call(s32[2]{0:T(128)} %pad_add_fusion.place, bf16[512,2048]{1,0:T(8,128)(2,1)} %get-tuple-element.59.h_ref, f32[512,2048]{1,0:T(8,128)} %shard_map.133.base_ref, bf16[512,2048]{1,0:T(8,128)(2,1)} %get-tuple-element.91.refs_0_, bf16[512,2048]{1,0:T(8,128)(2,1)} %collective-permute-done.25.refs_1_, ...), custom_call_target="tpu_custom_call" | custom-call | flops 12884901888 | bytes 29360128 | tf_op jit(solution)/shard_map/pallas_call | solution.py:283
  344.9 23.6 %shard_map.121.base_ref = f32[512,2048]{1,0:T(8,128)} custom-call(s32[2]{0:T(128)} %pad_add_fusion.place, bf16[512,2048]{1,0:T(8,128)(2,1)} %get-tuple-element.35.h_ref, bf16[512,512]{1,0:T(8,128)(2,1)} %attn.8.base_ref, bf16[512,2048]{1,0:T(8,128)(2,1)} %get-tuple-element.90.refs_0_, bf16[512,2048]{1,0:T(8,128)(2,1)} %collective-permute-done.5.refs_1_, ...), custom_call_target="tpu_custom_call" | custom-call | flops 12884901888 | bytes 29360128 | tf_op jit(solution)/shard_map/pallas_call | solution.py:283
  368.5 21.7 %shard_map.122 = bf16[512,2048]{1,0:T(8,128)(2,1)} custom-call(s32[2]{0:T(128)} %pad_add_fusion.place, bf16[512,2048]{1,0:T(8,128)(2,1)} %get-tuple-element.35.h_ref, f32[512,2048]{1,0:T(8,128)} %shard_map.121.base_ref, bf16[512,2048]{1,0:T(8,128)(2,1)} %get-tuple-element.91.refs_0_, bf16[512,2048]{1,0:T(8,128)(2,1)} %collective-permute-done.25.refs_1_, ...), custom_call_target="tpu_custom_call" | custom-call | flops 12884901888 | bytes 29360128 | tf_op jit(solution)/shard_map/pallas_call | solution.py:283
  394.8 23.8 %shard_map.125.base_ref = f32[512,2048]{1,0:T(8,128)} custom-call(s32[2]{0:T(128)} %pad_add_fusion.place, bf16[512,2048]{1,0:T(8,128)(2,1)} %get-tuple-element.43.h_ref, bf16[512,512]{1,0:T(8,128)(2,1)} %attn.10.base_ref, bf16[512,2048]{1,0:T(8,128)(2,1)} %get-tuple-element.90.refs_0_, bf16[512,2048]{1,0:T(8,128)(2,1)} %collective-permute-done.5.refs_1_, ...), custom_call_target="tpu_custom_call" | custom-call | flops 12884901888 | bytes 29360128 | tf_op jit(solution)/shard_map/pallas_call | solution.py:283
  418.5 21.7 %shard_map.126 = bf16[512,2048]{1,0:T(8,128)(2,1)} custom-call(s32[2]{0:T(128)} %pad_add_fusion.place, bf16[512,2048]{1,0:T(8,128)(2,1)} %get-tuple-element.43.h_ref, f32[512,2048]{1,0:T(8,128)} %shard_map.125.base_ref, bf16[512,2048]{1,0:T(8,128)(2,1)} %get-tuple-element.91.refs_0_, bf16[512,2048]{1,0:T(8,128)(2,1)} %collective-permute-done.25.refs_1_, ...), custom_call_target="tpu_custom_call" | custom-call | flops 12884901888 | bytes 29360128 | tf_op jit(solution)/shard_map/pallas_call | solution.py:283
  448.0 15.7 %collective-permute-done.66.refs_20_ = bf16[256,512]{1,0:T(8,128)(2,1)S(1)} collective-permute-done((bf16[256,512]{1,0:T(8,128)(2,1)S(1)}, bf16[256,512]{1,0:T(8,128)(2,1)S(1)}, u32[]{:S(2)}, u32[]{:S(2)}) %collective-permute-start.66) | collective-permute-done | bytes 262176 | tf_op jit(solution)/shard_map/ppermute | solution.py:311
  470.7 23.4 %shard_map.129.base_ref = f32[512,2048]{1,0:T(8,128)} custom-call(s32[2]{0:T(128)} %pad_add_fusion.place, bf16[512,2048]{1,0:T(8,128)(2,1)} %get-tuple-element.51.h_ref, bf16[512,512]{1,0:T(8,128)(2,1)} %attn.12.base_ref, bf16[512,2048]{1,0:T(8,128)(2,1)} %get-tuple-element.90.refs_0_, bf16[512,2048]{1,0:T(8,128)(2,1)} %collective-permute-done.5.refs_1_, ...), custom_call_target="tpu_custom_call" | custom-call | flops 12884901888 | bytes 29360128 | tf_op jit(solution)/shard_map/pallas_call | solution.py:283
  497.4 21.7 %shard_map.130 = bf16[512,2048]{1,0:T(8,128)(2,1)} custom-call(s32[2]{0:T(128)} %pad_add_fusion.place, bf16[512,2048]{1,0:T(8,128)(2,1)} %get-tuple-element.51.h_ref, f32[512,2048]{1,0:T(8,128)} %shard_map.129.base_ref, bf16[512,2048]{1,0:T(8,128)(2,1)} %get-tuple-element.91.refs_0_, bf16[512,2048]{1,0:T(8,128)(2,1)} %collective-permute-done.25.refs_1_, ...), custom_call_target="tpu_custom_call" | custom-call | flops 12884901888 | bytes 29360128 | tf_op jit(solution)/shard_map/pallas_call | solution.py:283
  527.5 15.5 %collective-permute-done.56.refs_8_ = bf16[256,2048]{1,0:T(8,128)(2,1)} collective-permute-done((bf16[256,2048]{1,0:T(8,128)(2,1)}, bf16[256,2048]{1,0:T(8,128)(2,1)}, u32[]{:S(2)}, u32[]{:S(2)}) %collective-permute-start.56) | collective-permute-done | bytes 1048608 | tf_op jit(solution)/shard_map/ppermute | solution.py:311
  544.5 20.9 %collective-permute-done.61.refs_14_ = bf16[1024,512]{1,0:T(8,128)(2,1)S(1)} collective-permute-done((bf16[1024,512]{1,0:T(8,128)(2,1)S(1)}, bf16[1024,512]{1,0:T(8,128)(2,1)S(1)}, u32[]{:S(2)}, u32[]{:S(2)}) %collective-permute-start.61) | collective-permute-done | bytes 1048608 | tf_op jit(solution)/shard_map/ppermute | solution.py:311
  566.3 21.6 %collective-permute-done.71.refs_2_ = bf16[256,2048]{1,0:T(8,128)(2,1)} collective-permute-done((bf16[256,2048]{1,0:T(8,128)(2,1)}, bf16[256,2048]{1,0:T(8,128)(2,1)}, u32[]{:S(2)}, u32[]{:S(2)}) %collective-permute-start.71) | collective-permute-done | bytes 1048608 | tf_op jit(solution)/shard_map/ppermute | solution.py:311
  589.5 20.9 %collective-permute-done.76.refs_8_ = bf16[256,2048]{1,0:T(8,128)(2,1)} collective-permute-done((bf16[256,2048]{1,0:T(8,128)(2,1)}, bf16[256,2048]{1,0:T(8,128)(2,1)}, u32[]{:S(2)}, u32[]{:S(2)}) %collective-permute-start.76) | collective-permute-done | bytes 1048608 | tf_op jit(solution)/shard_map/ppermute | solution.py:311
  610.9 21.5 %collective-permute-done.81.refs_14_ = bf16[1024,512]{1,0:T(8,128)(2,1)} collective-permute-done((bf16[1024,512]{1,0:T(8,128)(2,1)S(1)}, bf16[1024,512]{1,0:T(8,128)(2,1)}, u32[]{:S(2)}, u32[]{:S(2)}) %collective-permute-start.81) | collective-permute-done | bytes 1048608 | tf_op jit(solution)/shard_map/ppermute | solution.py:311
  668.0 9.3 collective-permute-done.99
  679.0 9.0 collective-permute-done.97
  691.2 14.3 %collective-permute-done.44 = bf16[128,2048]{1,0:T(8,128)(2,1)S(1)} collective-permute-done((bf16[128,2048]{1,0:T(8,128)(2,1)}, bf16[128,2048]{1,0:T(8,128)(2,1)S(1)}, u32[]{:S(2)}, u32[]{:S(2)}) %collective-permute-start.44) | collective-permute-done | bytes 524320 | tf_op jit(solution)/shard_map/ppermute | solution.py:325
  705.5 11.2 %collective-permute-done.42 = bf16[128,2048]{1,0:T(8,128)(2,1)S(1)} collective-permute-done((bf16[128,2048]{1,0:T(8,128)(2,1)}, bf16[128,2048]{1,0:T(8,128)(2,1)S(1)}, u32[]{:S(2)}, u32[]{:S(2)}) %collective-permute-start.42) | collective-permute-done | bytes 524320 | tf_op jit(solution)/shard_map/ppermute | solution.py:326
  732.4 7.7 qkv.15
  749.2 7.6 qkv.9
  768.4 14.0 %collective-permute-done.94 = bf16[128,2048]{1,0:T(8,128)(2,1)S(1)} collective-permute-done((bf16[128,2048]{1,0:T(8,128)(2,1)}, bf16[128,2048]{1,0:T(8,128)(2,1)S(1)}, u32[]{:S(2)}, u32[]{:S(2)}) %collective-permute-start.94) | collective-permute-done | bytes 524320 | tf_op jit(solution)/shard_map/ppermute | solution.py:325
  783.7 9.9 collective-permute-done.92
  795.1 7.6 qkv.11
  813.1 7.6 qkv.13
  832.9 23.6 %shard_map.135.base_ref = f32[512,2048]{1,0:T(8,128)} custom-call(s32[2]{0:T(128)} %pad_add_fusion.place, bf16[512,2048]{1,0:T(8,128)(2,1)} %get-tuple-element.63.h_ref, bf16[512,512]{1,0:T(8,128)(2,1)} %attn.15.base_ref, bf16[512,2048]{1,0:T(8,128)(2,1)} %get-tuple-element.92.refs_0_, bf16[512,2048]{1,0:T(8,128)(2,1)} %collective-permute-done.50.refs_1_, ...), custom_call_target="tpu_custom_call" | custom-call | flops 12884901888 | bytes 29360128 | tf_op jit(solution)/shard_map/pallas_call | solution.py:283
  856.6 21.7 %shard_map.136 = bf16[4,512,512]{2,1,0:T(8,128)(2,1)} custom-call(s32[2]{0:T(128)} %pad_add_fusion.place, bf16[512,2048]{1,0:T(8,128)(2,1)} %get-tuple-element.63.h_ref, f32[512,2048]{1,0:T(8,128)} %shard_map.135.base_ref, bf16[512,2048]{1,0:T(8,128)(2,1)} %get-tuple-element.93.refs_0_, bf16[512,2048]{1,0:T(8,128)(2,1)} %collective-permute-done.70.refs_1_, ...), custom_call_target="tpu_custom_call" | custom-call | flops 12884901888 | bytes 29360128 | tf_op jit(solution)/shard_map/pallas_call | solution.py:283
  884.0 23.4 %shard_map.131.base_ref = f32[512,2048]{1,0:T(8,128)} custom-call(s32[2]{0:T(128)} %pad_add_fusion.place, bf16[512,2048]{1,0:T(8,128)(2,1)} %get-tuple-element.55.h_ref, bf16[512,512]{1,0:T(8,128)(2,1)} %attn.13.base_ref, bf16[512,2048]{1,0:T(8,128)(2,1)} %get-tuple-element.92.refs_0_, bf16[512,2048]{1,0:T(8,128)(2,1)} %collective-permute-done.50.refs_1_, ...), custom_call_target="tpu_custom_call" | custom-call | flops 12884901888 | bytes 29360128 | tf_op jit(solution)/shard_map/pallas_call | solution.py:283
  907.4 21.8 %shard_map.132 = bf16[4,512,512]{2,1,0:T(8,128)(2,1)} custom-call(s32[2]{0:T(128)} %pad_add_fusion.place, bf16[512,2048]{1,0:T(8,128)(2,1)} %get-tuple-element.55.h_ref, f32[512,2048]{1,0:T(8,128)} %shard_map.131.base_ref, bf16[512,2048]{1,0:T(8,128)(2,1)} %get-tuple-element.93.refs_0_, bf16[512,2048]{1,0:T(8,128)(2,1)} %collective-permute-done.70.refs_1_, ...), custom_call_target="tpu_custom_call" | custom-call | flops 12884901888 | bytes 29360128 | tf_op jit(solution)/shard_map/pallas_call | solution.py:283
  933.8 23.4 %shard_map.127.base_ref = f32[512,2048]{1,0:T(8,128)} custom-call(s32[2]{0:T(128)} %pad_add_fusion.place, bf16[512,2048]{1,0:T(8,128)(2,1)} %get-tuple-element.47.h_ref, bf16[512,512]{1,0:T(8,128)(2,1)} %attn.11.base_ref, bf16[512,2048]{1,0:T(8,128)(2,1)} %get-tuple-element.92.refs_0_, bf16[512,2048]{1,0:T(8,128)(2,1)} %collective-permute-done.50.refs_1_, ...), custom_call_target="tpu_custom_call" | custom-call | flops 12884901888 | bytes 29360128 | tf_op jit(solution)/shard_map/pallas_call | solution.py:283
  957.2 21.8 %shard_map.128 = bf16[4,512,512]{2,1,0:T(8,128)(2,1)} custom-call(s32[2]{0:T(128)} %pad_add_fusion.place, bf16[512,2048]{1,0:T(8,128)(2,1)} %get-tuple-element.47.h_ref, f32[512,2048]{1,0:T(8,128)} %shard_map.127.base_ref, bf16[512,2048]{1,0:T(8,128)(2,1)} %get-tuple-element.93.refs_0_, bf16[512,2048]{1,0:T(8,128)(2,1)} %collective-permute-done.70.refs_1_, ...), custom_call_target="tpu_custom_call" | custom-call | flops 12884901888 | bytes 29360128 | tf_op jit(solution)/shard_map/pallas_call | solution.py:283
  982.6 23.4 %shard_map.123.base_ref = f32[512,2048]{1,0:T(8,128)} custom-call(s32[2]{0:T(128)} %pad_add_fusion.place, bf16[512,2048]{1,0:T(8,128)(2,1)} %get-tuple-element.39.h_ref, bf16[512,512]{1,0:T(8,128)(2,1)} %attn.9.base_ref, bf16[512,2048]{1,0:T(8,128)(2,1)} %get-tuple-element.92.refs_0_, bf16[512,2048]{1,0:T(8,128)(2,1)} %collective-permute-done.50.refs_1_, ...), custom_call_target="tpu_custom_call" | custom-call | flops 12884901888 | bytes 29360128 | tf_op jit(solution)/shard_map/pallas_call | solution.py:283
  1006.0 21.8 %shard_map.124 = bf16[4,512,512]{2,1,0:T(8,128)(2,1)} custom-call(s32[2]{0:T(128)} %pad_add_fusion.place, bf16[512,2048]{1,0:T(8,128)(2,1)} %get-tuple-element.39.h_ref, f32[512,2048]{1,0:T(8,128)} %shard_map.123.base_ref, bf16[512,2048]{1,0:T(8,128)(2,1)} %get-tuple-element.93.refs_0_, bf16[512,2048]{1,0:T(8,128)(2,1)} %collective-permute-done.70.refs_1_, ...), custom_call_target="tpu_custom_call" | custom-call | flops 12884901888 | bytes 29360128 | tf_op jit(solution)/shard_map/pallas_call | solution.py:283
  1037.8 43.6 %reduce-scatter.11.cloned.1.call-done = bf16[1,512,512]{2,1,0:T(8,128)(2,1)} async-done(((bf16[4,512,512]{2,1,0:T(8,128)(2,1)}), bf16[1,512,512]{2,1,0:T(8,128)(2,1)}) %reduce-scatter.11.cloned.1.call-update) | async-done | bytes 524304 | tf_op jit(solution)/shard_map/reduce_scatter | solution.py:398
  (379 shorter events, 244.6 us)
Async XLA Ops:
  7.2 223.6 %all-gather.11.cloned.1.call-start = ((), (), s32[]{:S(2)}) async-start(), calls=%async_computation.17 | async-start | bytes 2621440 | tf_op jit(solution)/shard_map/all_gather | solution.py:355
  10.2 228.2 %all-gather.5.cloned.1.call-start = ((), (), s32[]{:S(2)}) async-start(), calls=%async_computation.8 | async-start | bytes 2621440 | tf_op jit(solution)/shard_map/all_gather | solution.py:355
  11.0 261.9 %all-gather.7.cloned.1.call-start = ((), (), s32[]{:S(2)}) async-start(), calls=%async_computation.11 | async-start | bytes 2621440 | tf_op jit(solution)/shard_map/all_gather | solution.py:355
  13.6 45.6 %collective-permute-start = (bf16[512,1024]{1,0:T(8,128)(2,1)S(1)}, bf16[512,1024]{1,0:T(8,128)(2,1)}, u32[]{:S(2)}, u32[]{:S(2)}) collective-permute-start(bf16[512,1024]{1,0:T(8,128)(2,1)S(1)} %pad_maximum_fusion.4.refs_0_), channel_id=1, source_target_pairs={{0,1},{1,0},{2,3},{3,2},{4,5},{5,4},{6,7},{7,6},{8,9},{9,8},{10,11... | collective-permute-start | bytes 3145736 | tf_op jit(solution)/shard_map/ppermute | solution.py:313
  18.6 36.7 %collective-permute-start.20 = (bf16[512,512]{1,0:T(8,128)(2,1)}, bf16[512,512]{1,0:T(8,128)(2,1)}, u32[]{:S(2)}, u32[]{:S(2)}) collective-permute-start(bf16[512,512]{1,0:T(8,128)(2,1)} %bitcast.11.refs_18_), channel_id=1, source_target_pairs={{0,1},{1,0},{2,3},{3,2},{4,5},{5,4},{6,7},{7,6},{8,9},{9,8},{10,11... | collective-permute-start | bytes 1572872 | tf_op jit(solution)/shard_map/ppermute | solution.py:313
  29.4 42.2 %collective-permute-start.6 = (bf16[256,2048]{1,0:T(8,128)(2,1)}, bf16[256,2048]{1,0:T(8,128)(2,1)}, u32[]{:S(2)}, u32[]{:S(2)}) collective-permute-start(bf16[256,2048]{1,0:T(8,128)(2,1)} %dynamic-slice_bitcast_fusion.11), channel_id=1, source_target_pairs={{0,2},{1,3},{2,0},{3,1},{4,6},{5,7},{6,4},{7,5},{8,10},{9,11},{10,... | collective-permute-start | bytes 3145736 | tf_op jit(solution)/shard_map/ppermute | solution.py:311
  31.1 249.5 %all-gather.9.cloned.1.call-start = ((), (), s32[]{:S(2)}) async-start(), calls=%async_computation.14 | async-start | bytes 2621440 | tf_op jit(solution)/shard_map/all_gather | solution.py:355
  59.2 118.1 %collective-permute-start.5 = (bf16[512,2048]{1,0:T(8,128)(2,1)}, bf16[512,2048]{1,0:T(8,128)(2,1)}, u32[]{:S(2)}, u32[]{:S(2)}) collective-permute-start(bf16[512,2048]{1,0:T(8,128)(2,1)} %get-tuple-element.90.refs_0_), channel_id=1, source_target_pairs={{0,1},{1,0},{2,3},{3,2},{4,5},{5,4},{6,7},{7,6},{8,9},{9,8},{10,11... | collective-permute-start | bytes 6291464 | tf_op jit(solution)/shard_map/ppermute | solution.py:313
  69.5 36.1 %collective-permute-start.16 = (bf16[1024,512]{1,0:T(8,128)(2,1)S(1)}, bf16[1024,512]{1,0:T(8,128)(2,1)S(1)}, u32[]{:S(2)}, u32[]{:S(2)}) collective-permute-start(bf16[1024,512]{1,0:T(8,128)(2,1)S(1)} %dynamic-slice_bitcast_fusion.9), channel_id=1, source_target_pairs={{0,2},{1,3},{2,0},{3,1},{4,6},{5,7},{6,4},{7,5},{8,10},{9,11},{10,... | collective-permute-start | bytes 3145736 | tf_op jit(solution)/shard_map/ppermute | solution.py:311
  71.0 57.1 %collective-permute-start.26 = (bf16[256,2048]{1,0:T(8,128)(2,1)S(1)}, bf16[256,2048]{1,0:T(8,128)(2,1)}, u32[]{:S(2)}, u32[]{:S(2)}) collective-permute-start(bf16[256,2048]{1,0:T(8,128)(2,1)S(1)} %dynamic-slice_bitcast_fusion.8), channel_id=1, source_target_pairs={{0,2},{1,3},{2,0},{3,1},{4,6},{5,7},{6,4},{7,5},{8,10},{9,11},{10,... | collective-permute-start | bytes 3145736 | tf_op jit(solution)/shard_map/ppermute | solution.py:311
  71.7 79.0 %collective-permute-start.31 = (bf16[256,2048]{1,0:T(8,128)(2,1)S(1)}, bf16[256,2048]{1,0:T(8,128)(2,1)}, u32[]{:S(2)}, u32[]{:S(2)}) collective-permute-start(bf16[256,2048]{1,0:T(8,128)(2,1)S(1)} %dynamic-slice_bitcast_fusion.7), channel_id=1, source_target_pairs={{0,2},{1,3},{2,0},{3,1},{4,6},{5,7},{6,4},{7,5},{8,10},{9,11},{10,... | collective-permute-start | bytes 3145736 | tf_op jit(solution)/shard_map/ppermute | solution.py:311
  83.2 89.5 %collective-permute-start.36 = (bf16[1024,512]{1,0:T(8,128)(2,1)S(1)}, bf16[1024,512]{1,0:T(8,128)(2,1)S(1)}, u32[]{:S(2)}, u32[]{:S(2)}) collective-permute-start(bf16[1024,512]{1,0:T(8,128)(2,1)S(1)} %dynamic-slice_bitcast_fusion.6), channel_id=1, source_target_pairs={{0,2},{1,3},{2,0},{3,1},{4,6},{5,7},{6,4},{7,5},{8,10},{9,11},{10,... | collective-permute-start | bytes 3145736 | tf_op jit(solution)/shard_map/ppermute | solution.py:311
  105.6 72.4 %collective-permute-start.10 = (bf16[512,2048]{1,0:T(8,128)(2,1)}, bf16[512,2048]{1,0:T(8,128)(2,1)}, u32[]{:S(2)}, u32[]{:S(2)}) collective-permute-start(bf16[512,2048]{1,0:T(8,128)(2,1)} %get-tuple-element.82.refs_6_), channel_id=1, source_target_pairs={{0,1},{1,0},{2,3},{3,2},{4,5},{5,4},{6,7},{7,6},{8,9},{9,8},{10,11... | collective-permute-start | bytes 6291464 | tf_op jit(solution)/shard_map/ppermute | solution.py:313
  128.2 49.1 %collective-permute-start.7 = (bf16[256,2048]{1,0:T(8,128)(2,1)}, bf16[256,2048]{1,0:T(8,128)(2,1)}, u32[]{:S(2)}, u32[]{:S(2)}) collective-permute-start(bf16[256,2048]{1,0:T(8,128)(2,1)} %collective-permute-done.6.refs_2_), channel_id=1, source_target_pairs={{0,16},{16,0},{1,17},{17,1},{2,18},{18,2},{3,19},{19,3},{4,20},{20... | collective-permute-start | bytes 3145736 | tf_op jit(solution)/shard_map/ppermute | solution.py:312
  177.3 45.7 %collective-permute-start.15 = (bf16[2048,512]{1,0:T(8,128)(2,1)}, bf16[2048,512]{1,0:T(8,128)(2,1)}, u32[]{:S(2)}, u32[]{:S(2)}) collective-permute-start(bf16[2048,512]{1,0:T(8,128)(2,1)} %get-tuple-element.74.refs_12_), channel_id=1, source_target_pairs={{0,1},{1,0},{2,3},{3,2},{4,5},{5,4},{6,7},{7,6},{8,9},{9,8},{10,11... | collective-permute-start | bytes 6291464 | tf_op jit(solution)/shard_map/ppermute | solution.py:313
  177.8 51.4 %collective-permute-start.25 = (bf16[512,2048]{1,0:T(8,128)(2,1)}, bf16[512,2048]{1,0:T(8,128)(2,1)}, u32[]{:S(2)}, u32[]{:S(2)}) collective-permute-start(bf16[512,2048]{1,0:T(8,128)(2,1)} %get-tuple-element.91.refs_0_), channel_id=1, source_target_pairs={{0,1},{1,0},{2,3},{3,2},{4,5},{5,4},{6,7},{7,6},{8,9},{9,8},{10,11... | collective-permute-start | bytes 6291464 | tf_op jit(solution)/shard_map/ppermute | solution.py:313
  177.9 454.5 %reduce-scatter.21.cloned.1.call-start = ((), (), s32[]{:S(2)}) async-start(), calls=%async_computation.18 | async-start | bytes 2621440 | tf_op jit(solution)/shard_map/reduce_scatter | solution.py:388
  178.0 73.7 %collective-permute-start.30 = (bf16[512,2048]{1,0:T(8,128)(2,1)}, bf16[512,2048]{1,0:T(8,128)(2,1)}, u32[]{:S(2)}, u32[]{:S(2)}) collective-permute-start(bf16[512,2048]{1,0:T(8,128)(2,1)} %get-tuple-element.83.refs_6_), channel_id=1, source_target_pairs={{0,1},{1,0},{2,3},{3,2},{4,5},{5,4},{6,7},{7,6},{8,9},{9,8},{10,11... | collective-permute-start | bytes 6291464 | tf_op jit(solution)/shard_map/ppermute | solution.py:313
  227.5 44.9 %collective-permute-start.32 = (bf16[256,2048]{1,0:T(8,128)(2,1)}, bf16[256,2048]{1,0:T(8,128)(2,1)}, u32[]{:S(2)}, u32[]{:S(2)}) collective-permute-start(bf16[256,2048]{1,0:T(8,128)(2,1)} %collective-permute-done.31.refs_8_), channel_id=1, source_target_pairs={{0,16},{16,0},{1,17},{17,1},{2,18},{18,2},{3,19},{19,3},{4,20},{20... | collective-permute-start | bytes 3145736 | tf_op jit(solution)/shard_map/ppermute | solution.py:312
  229.2 43.2 %collective-permute-start.33 = (bf16[256,2048]{1,0:T(8,128)(2,1)}, bf16[256,2048]{1,0:T(8,128)(2,1)}, u32[]{:S(2)}, u32[]{:S(2)}) collective-permute-start(bf16[256,2048]{1,0:T(8,128)(2,1)} %collective-permute-done.31.refs_8_), channel_id=1, source_target_pairs={{0,1},{1,0},{2,3},{3,2},{4,5},{5,4},{6,7},{7,6},{8,9},{9,8},{10,11... | collective-permute-start | bytes 3145736 | tf_op jit(solution)/shard_map/ppermute | solution.py:314
  249.9 69.4 %collective-permute-start.35 = (bf16[2048,512]{1,0:T(8,128)(2,1)}, bf16[2048,512]{1,0:T(8,128)(2,1)}, u32[]{:S(2)}, u32[]{:S(2)}) collective-permute-start(bf16[2048,512]{1,0:T(8,128)(2,1)} %get-tuple-element.75.refs_12_), channel_id=1, source_target_pairs={{0,1},{1,0},{2,3},{3,2},{4,5},{5,4},{6,7},{7,6},{8,9},{9,8},{10,11... | collective-permute-start | bytes 6291464 | tf_op jit(solution)/shard_map/ppermute | solution.py:313
  249.9 45.1 %collective-permute-start.37 = (bf16[1024,512]{1,0:T(8,128)(2,1)S(1)}, bf16[1024,512]{1,0:T(8,128)(2,1)}, u32[]{:S(2)}, u32[]{:S(2)}) collective-permute-start(bf16[1024,512]{1,0:T(8,128)(2,1)S(1)} %copy-done.38), channel_id=1, source_target_pairs={{0,16},{16,0},{1,17},{17,1},{2,18},{18,2},{3,19},{19,3},{4,20},{20... | collective-permute-start | bytes 3145736 | tf_op jit(solution)/shard_map/ppermute | solution.py:312
  251.7 43.4 %collective-permute-start.9 = (bf16[256,2048]{1,0:T(8,128)(2,1)}, bf16[256,2048]{1,0:T(8,128)(2,1)}, u32[]{:S(2)}, u32[]{:S(2)}) collective-permute-start(bf16[256,2048]{1,0:T(8,128)(2,1)} %collective-permute-done.7.refs_3_), channel_id=1, source_target_pairs={{0,1},{1,0},{2,3},{3,2},{4,5},{5,4},{6,7},{7,6},{8,9},{9,8},{10,11... | collective-permute-start | bytes 3145736 | tf_op jit(solution)/shard_map/ppermute | solution.py:315
  341.3 297.0 %reduce-scatter.9.cloned.1.call-start = ((), (), s32[]{:S(2)}) async-start(), calls=%async_computation.9 | async-start | bytes 2621440 | tf_op jit(solution)/shard_map/reduce_scatter | solution.py:388
  390.3 274.1 %reduce-scatter.13.cloned.1.call-start = ((), (), s32[]{:S(2)}) async-start(), calls=%async_computation.12 | async-start | bytes 2621440 | tf_op jit(solution)/shard_map/reduce_scatter | solution.py:388
  440.3 226.5 %reduce-scatter.17.cloned.1.call-start = ((), (), s32[]{:S(2)}) async-start(), calls=%async_computation.15 | async-start | bytes 2621440 | tf_op jit(solution)/shard_map/reduce_scatter | solution.py:388
  442.6 78.7 %collective-permute-start.45 = (bf16[512,1024]{1,0:T(8,128)(2,1)S(1)}, bf16[512,1024]{1,0:T(8,128)(2,1)}, u32[]{:S(2)}, u32[]{:S(2)}) collective-permute-start(bf16[512,1024]{1,0:T(8,128)(2,1)S(1)} %pad_maximum_fusion.5.refs_0_), channel_id=1, source_target_pairs={{0,1},{1,0},{2,3},{3,2},{4,5},{5,4},{6,7},{7,6},{8,9},{9,8},{10,11... | collective-permute-start | bytes 3145736 | tf_op jit(solution)/shard_map/ppermute | solution.py:313
  443.6 50.5 %collective-permute-start.46 = (bf16[256,1024]{1,0:T(8,128)(2,1)}, bf16[256,1024]{1,0:T(8,128)(2,1)}, u32[]{:S(2)}, u32[]{:S(2)}) collective-permute-start(bf16[256,1024]{1,0:T(8,128)(2,1)} %constant_dynamic-slice_fusion.1), channel_id=1, source_target_pairs={{0,2},{1,3},{2,0},{3,1},{4,6},{5,7},{6,4},{7,5},{8,10},{9,11},{10,... | collective-permute-start | bytes 1572872 | tf_op jit(solution)/shard_map/ppermute | solution.py:311
  445.4 50.3 %collective-permute-start.65 = (bf16[512,512]{1,0:T(8,128)(2,1)S(1)}, bf16[512,512]{1,0:T(8,128)(2,1)}, u32[]{:S(2)}, u32[]{:S(2)}) collective-permute-start(bf16[512,512]{1,0:T(8,128)(2,1)S(1)} %bitcast.124), channel_id=1, source_target_pairs={{0,1},{1,0},{2,3},{3,2},{4,5},{5,4},{6,7},{7,6},{8,9},{9,8},{10,11... | collective-permute-start | bytes 1572872 | tf_op jit(solution)/shard_map/ppermute | solution.py:313
  495.7 47.3 %collective-permute-start.56 = (bf16[256,2048]{1,0:T(8,128)(2,1)}, bf16[256,2048]{1,0:T(8,128)(2,1)}, u32[]{:S(2)}, u32[]{:S(2)}) collective-permute-start(bf16[256,2048]{1,0:T(8,128)(2,1)} %dynamic-slice_bitcast_fusion.4), channel_id=1, source_target_pairs={{0,2},{1,3},{2,0},{3,1},{4,6},{5,7},{6,4},{7,5},{8,10},{9,11},{10,... | collective-permute-start | bytes 3145736 | tf_op jit(solution)/shard_map/ppermute | solution.py:311
  519.2 514.6 %reduce-scatter.23.cloned.1.call-start = ((), (), s32[]{:S(2)}) async-start(), calls=%async_computation.19 | async-start | bytes 2621440 | tf_op jit(solution)/shard_map/reduce_scatter | solution.py:398
  521.3 113.6 %collective-permute-start.50 = (bf16[512,2048]{1,0:T(8,128)(2,1)}, bf16[512,2048]{1,0:T(8,128)(2,1)}, u32[]{:S(2)}, u32[]{:S(2)}) collective-permute-start(bf16[512,2048]{1,0:T(8,128)(2,1)} %get-tuple-element.92.refs_0_), channel_id=1, source_target_pairs={{0,1},{1,0},{2,3},{3,2},{4,5},{5,4},{6,7},{7,6},{8,9},{9,8},{10,11... | collective-permute-start | bytes 6291464 | tf_op jit(solution)/shard_map/ppermute | solution.py:313
  521.4 44.0 %collective-permute-start.61 = (bf16[1024,512]{1,0:T(8,128)(2,1)S(1)}, bf16[1024,512]{1,0:T(8,128)(2,1)S(1)}, u32[]{:S(2)}, u32[]{:S(2)}) collective-permute-start(bf16[1024,512]{1,0:T(8,128)(2,1)S(1)} %dynamic-slice_bitcast_fusion.3), channel_id=1, source_target_pairs={{0,2},{1,3},{2,0},{3,1},{4,6},{5,7},{6,4},{7,5},{8,10},{9,11},{10,... | collective-permute-start | bytes 3145736 | tf_op jit(solution)/shard_map/ppermute | solution.py:311
  524.2 63.8 %collective-permute-start.71 = (bf16[256,2048]{1,0:T(8,128)(2,1)}, bf16[256,2048]{1,0:T(8,128)(2,1)}, u32[]{:S(2)}, u32[]{:S(2)}) collective-permute-start(bf16[256,2048]{1,0:T(8,128)(2,1)} %dynamic-slice_bitcast_fusion.2), channel_id=1, source_target_pairs={{0,2},{1,3},{2,0},{3,1},{4,6},{5,7},{6,4},{7,5},{8,10},{9,11},{10,... | collective-permute-start | bytes 3145736 | tf_op jit(solution)/shard_map/ppermute | solution.py:311
  525.7 84.8 %collective-permute-start.76 = (bf16[256,2048]{1,0:T(8,128)(2,1)}, bf16[256,2048]{1,0:T(8,128)(2,1)}, u32[]{:S(2)}, u32[]{:S(2)}) collective-permute-start(bf16[256,2048]{1,0:T(8,128)(2,1)} %dynamic-slice_bitcast_fusion.1), channel_id=1, source_target_pairs={{0,2},{1,3},{2,0},{3,1},{4,6},{5,7},{6,4},{7,5},{8,10},{9,11},{10,... | collective-permute-start | bytes 3145736 | tf_op jit(solution)/shard_map/ppermute | solution.py:311
  543.0 89.4 %collective-permute-start.81 = (bf16[1024,512]{1,0:T(8,128)(2,1)S(1)}, bf16[1024,512]{1,0:T(8,128)(2,1)}, u32[]{:S(2)}, u32[]{:S(2)}) collective-permute-start(bf16[1024,512]{1,0:T(8,128)(2,1)S(1)} %dynamic-slice_bitcast_fusion), channel_id=1, source_target_pairs={{0,2},{1,3},{2,0},{3,1},{4,6},{5,7},{6,4},{7,5},{8,10},{9,11},{10,... | collective-permute-start | bytes 3145736 | tf_op jit(solution)/shard_map/ppermute | solution.py:311
  566.3 85.1 %collective-permute-start.55 = (bf16[512,2048]{1,0:T(8,128)(2,1)}, bf16[512,2048]{1,0:T(8,128)(2,1)}, u32[]{:S(2)}, u32[]{:S(2)}) collective-permute-start(bf16[512,2048]{1,0:T(8,128)(2,1)} %get-tuple-element.84.refs_6_), channel_id=1, source_target_pairs={{0,1},{1,0},{2,3},{3,2},{4,5},{5,4},{6,7},{7,6},{8,9},{9,8},{10,11... | collective-permute-start | bytes 6291464 | tf_op jit(solution)/shard_map/ppermute | solution.py:313
  587.9 46.5 %collective-permute-start.49 = (bf16[256,1024]{1,0:T(8,128)(2,1)}, bf16[256,1024]{1,0:T(8,128)(2,1)}, u32[]{:S(2)}, u32[]{:S(2)}) collective-permute-start(bf16[256,1024]{1,0:T(8,128)(2,1)} %collective-permute-done.47.refs_3_), channel_id=1, source_target_pairs={{0,1},{1,0},{2,3},{3,2},{4,5},{5,4},{6,7},{7,6},{8,9},{9,8},{10,11... | collective-permute-start | bytes 1572872 | tf_op jit(solution)/shard_map/ppermute | solution.py:315
  660.3 60.5 %collective-permute-start.60 = (bf16[2048,512]{1,0:T(8,128)(2,1)}, bf16[2048,512]{1,0:T(8,128)(2,1)}, u32[]{:S(2)}, u32[]{:S(2)}) collective-permute-start(bf16[2048,512]{1,0:T(8,128)(2,1)} %get-tuple-element.76.refs_12_), channel_id=1, source_target_pairs={{0,1},{1,0},{2,3},{3,2},{4,5},{5,4},{6,7},{7,6},{8,9},{9,8},{10,11... | collective-permute-start | bytes 6291464 | tf_op jit(solution)/shard_map/ppermute | solution.py:313
  677.3 45.6 %collective-permute-start.62 = (bf16[1024,512]{1,0:T(8,128)(2,1)}, bf16[1024,512]{1,0:T(8,128)(2,1)}, u32[]{:S(2)}, u32[]{:S(2)}) collective-permute-start(bf16[1024,512]{1,0:T(8,128)(2,1)} %copy-done.36), channel_id=1, source_target_pairs={{0,16},{16,0},{1,17},{17,1},{2,18},{18,2},{3,19},{19,3},{4,20},{20... | collective-permute-start | bytes 3145736 | tf_op jit(solution)/shard_map/ppermute | solution.py:312
  691.1 77.3 %collective-permute-start.70 = (bf16[512,2048]{1,0:T(8,128)(2,1)S(1)}, bf16[512,2048]{1,0:T(8,128)(2,1)}, u32[]{:S(2)}, u32[]{:S(2)}) collective-permute-start(bf16[512,2048]{1,0:T(8,128)(2,1)S(1)} %copy-done.10), channel_id=1, source_target_pairs={{0,1},{1,0},{2,3},{3,2},{4,5},{5,4},{6,7},{7,6},{8,9},{9,8},{10,11... | collective-permute-start | bytes 6291464 | tf_op jit(solution)/shard_map/ppermute | solution.py:313
  749.2 57.3 %collective-permute-start.75 = (bf16[512,2048]{1,0:T(8,128)(2,1)}, bf16[512,2048]{1,0:T(8,128)(2,1)}, u32[]{:S(2)}, u32[]{:S(2)}) collective-permute-start(bf16[512,2048]{1,0:T(8,128)(2,1)} %get-tuple-element.85.refs_6_), channel_id=1, source_target_pairs={{0,1},{1,0},{2,3},{3,2},{4,5},{5,4},{6,7},{7,6},{8,9},{9,8},{10,11... | collective-permute-start | bytes 6291464 | tf_op jit(solution)/shard_map/ppermute | solution.py:313
  767.0 37.3 %collective-permute-start.72 = (bf16[256,2048]{1,0:T(8,128)(2,1)}, bf16[256,2048]{1,0:T(8,128)(2,1)}, u32[]{:S(2)}, u32[]{:S(2)}) collective-permute-start(bf16[256,2048]{1,0:T(8,128)(2,1)} %collective-permute-done.71.refs_2_), channel_id=1, source_target_pairs={{0,16},{16,0},{1,17},{17,1},{2,18},{18,2},{3,19},{19,3},{4,20},{20... | collective-permute-start | bytes 3145736 | tf_op jit(solution)/shard_map/ppermute | solution.py:312
  768.4 36.8 %collective-permute-start.73 = (bf16[256,2048]{1,0:T(8,128)(2,1)}, bf16[256,2048]{1,0:T(8,128)(2,1)}, u32[]{:S(2)}, u32[]{:S(2)}) collective-permute-start(bf16[256,2048]{1,0:T(8,128)(2,1)} %collective-permute-done.71.refs_2_), channel_id=1, source_target_pairs={{0,1},{1,0},{2,3},{3,2},{4,5},{5,4},{6,7},{7,6},{8,9},{9,8},{10,11... | collective-permute-start | bytes 3145736 | tf_op jit(solution)/shard_map/ppermute | solution.py:314
  804.7 51.9 %collective-permute-start.80 = (bf16[2048,512]{1,0:T(8,128)(2,1)S(1)}, bf16[2048,512]{1,0:T(8,128)(2,1)}, u32[]{:S(2)}, u32[]{:S(2)}) collective-permute-start(bf16[2048,512]{1,0:T(8,128)(2,1)S(1)} %copy-done.11), channel_id=1, source_target_pairs={{0,1},{1,0},{2,3},{3,2},{4,5},{5,4},{6,7},{7,6},{8,9},{9,8},{10,11... | collective-permute-start | bytes 6291464 | tf_op jit(solution)/shard_map/ppermute | solution.py:313
  878.3 156.8 %reduce-scatter.19.cloned.1.call-start = ((), (), s32[]{:S(2)}) async-start(), calls=%async_computation.16 | async-start | bytes 2621440 | tf_op jit(solution)/shard_map/reduce_scatter | solution.py:398
  929.2 107.2 %reduce-scatter.15.cloned.1.call-start = ((), (), s32[]{:S(2)}) async-start(), calls=%async_computation.13 | async-start | bytes 2621440 | tf_op jit(solution)/shard_map/reduce_scatter | solution.py:398
  979.0 102.4 %reduce-scatter.11.cloned.1.call-start = ((), (), s32[]{:S(2)}) async-start(), calls=%async_computation.10 | async-start | bytes 2621440 | tf_op jit(solution)/shard_map/reduce_scatter | solution.py:398
  (112 other events, 1956.4 us)
Sparse Core Ops, SparseCore 0:
  10.3 48.3 all-gather.10
  60.3 44.4 all-gather.4
  106.4 44.4 all-gather.6
  178.0 46.3 all-gather.8
  341.4 44.9 reduce-scatter.20
  390.4 44.7 reduce-scatter.8
  440.4 44.6 reduce-scatter.12
  519.3 44.9 reduce-scatter.16
  878.4 53.1 reduce-scatter.22
  933.7 48.6 reduce-scatter.18
  984.7 47.6 reduce-scatter.14
  1034.6 46.8 reduce-scatter.10
